TPU v7x, 128 devices: a whole 4x4x4 slice. The times are simulated.
128 devices in a mesh: head: 4 (over y_hi, core), seq: 32 (over x, z, y_lo).
Axes of the slice: x: 4, y: 4 (y_hi: 2, y_lo: 2; y = y_hi * 2 + y_lo), z: 4, core: 2. Of those that a mesh axis runs over, the one named last changes fastest.
Arguments:
- queries: bfloat16 [32768, 4096], P('seq', 'head'), may hold values from -6 to 6
- keys: bfloat16 [32768, 512], P('seq', 'head'), may hold values from -6 to 6
- values: bfloat16 [32768, 512], P('seq', 'head'), may hold values from -6 to 6
- vertical: int32 [32, 8], P('head'), may hold values from 0 to 255, as said below
- slash: int32 [32, 8], P('head'), may hold values from 1 to 28, as said below
Outputs:
- attended: bfloat16 [32768, 4096], P(('seq', 'head'))
Inputs may be any that keep to these rules, and one draw needn't show every extreme that they name: `vertical`: each row names 8 different blocks. Within each group of 8 consecutive rows, the different blocks named that lie in one slab (blocks s * 8 to s * 8 + 7) number at most 4, and exactly 4 in some slab. `slash`: each row names 8 different offsets.
All inputs are finite; a program needn't handle non-finite values.
Results may differ from a plain program's by a relative error of at most 0.0033.
Values may be sent and summed in bfloat16 or wider, within the bound.
No kernel may reach another device: no remote copies, remote signals or barrier semaphores. Data moves between devices by JAX's collectives and lax.ppermute only.
A program may use at most 128 MiB of HBM per device.

v0:
```python
import functools
import math

import jax
import jax.numpy as jnp
from jax import lax
from jax.experimental import pallas as pl
from jax.experimental.pallas import tpu as pltpu
from jax.sharding import Mesh
from jax.sharding import PartitionSpec as P

BLK = 128
HD = 128
REACH = 28
CAP = 4
NEG = -1e30
SEQ = ("x", "z", "y")
SCALE2 = math.log2(math.e) / math.sqrt(HD)


def cost(row_blocks, moved):
    return pl.CostEstimate(flops=row_blocks * 4 * BLK * HD, bytes_accessed=moved, transcendentals=row_blocks * BLK)


def prep_kernel(flat_ref, base_ref, keys_ref, values_ref, kv_ref, packed_ref):
    slab_blocks = kv_ref.shape[0]
    base = base_ref[0]

    def mark(entry, bits):
        local = flat_ref[entry] - base
        inside = (local >= 0) & (local < slab_blocks)
        return bits | jnp.where(inside, 1 << jnp.where(inside, local, 0), 0)

    bits = lax.fori_loop(0, flat_ref.shape[0], mark, jnp.int32(0))
    packed_ref[...] = jnp.zeros(packed_ref.shape, packed_ref.dtype)
    rank = jnp.int32(0)
    for block in range(slab_blocks):
        rows = pl.ds(block * BLK, BLK)
        kv_ref[block, :BLK, :] = keys_ref[rows, :].T
        kv_ref[block, BLK:, :] = values_ref[rows, :]
        used = (bits >> block) & 1

        @pl.when((used == 1) & (rank < CAP))
        def _(block=block, rank=rank):
            packed_ref[rank] = kv_ref[block]

        rank = rank + used


def prep(flat, base, keys, values):
    slab_blocks = keys.shape[0] // BLK
    whole = lambda shape: pl.BlockSpec(shape, lambda *_: (0,) * len(shape))
    return pl.pallas_call(
        prep_kernel,
        grid_spec=pltpu.PrefetchScalarGridSpec(
            num_scalar_prefetch=2,
            grid=(1,),
            in_specs=[whole(keys.shape), whole(values.shape)],
            out_specs=[whole((slab_blocks, 2 * BLK, HD)), whole((CAP, 2 * BLK, HD))],
        ),
        out_shape=[
            jax.ShapeDtypeStruct((slab_blocks, 2 * BLK, HD), jnp.bfloat16),
            jax.ShapeDtypeStruct((CAP, 2 * BLK, HD), jnp.bfloat16),
        ],
        name="prep",
    )(flat, base, keys, values)


def bias_columns(flags, rows):
    lanes = lax.broadcasted_iota(jnp.int32, (8, HD), 1)
    columns = jnp.zeros((8, HD), jnp.float32)
    for n, flag in enumerate(flags):
        columns = jnp.where(lanes == n, jnp.where(flag, 0.0, NEG).astype(jnp.float32), columns)
    return jnp.broadcast_to(columns[:1], (rows, HD)).astype(jnp.bfloat16)


def marker_rows(n):
    return (lax.broadcasted_iota(jnp.int32, (HD, BLK), 0) == n).astype(jnp.bfloat16)


def score_stage(q, flags, kts, score_ref, top_ref, causal=None, floor=None):
    left = jnp.concatenate([q, bias_columns(flags, q.shape[0])], axis=1)
    right = jnp.concatenate(
        [jnp.concatenate([kt, marker_rows(n)], axis=0) for n, kt in enumerate(kts)], axis=1
    )
    scores = jnp.dot(left, right, preferred_element_type=jnp.float32)
    parts = [scores[:, n * BLK : (n + 1) * BLK] * SCALE2 for n in range(len(kts))]
    if causal is not None:
        parts[0] = jnp.where(causal, parts[0], NEG)
    for n, part in enumerate(parts):
        score_ref[:, n * BLK : (n + 1) * BLK] = part
    top = jnp.max(functools.reduce(jnp.maximum, parts), axis=1, keepdims=True)
    if floor is not None:
        top = jnp.maximum(top, floor)
    top_ref[...] = jnp.broadcast_to(top, top_ref.shape)


def weight_stage(score_ref, top_ref, vs):
    top = top_ref[...]
    rounded = []
    for n in range(len(vs)):
        weights = jnp.exp2(score_ref[:, n * BLK : (n + 1) * BLK] - top)
        rounded.append(weights.astype(jnp.bfloat16))
    v = jnp.concatenate(vs, axis=0)
    v = jnp.concatenate([v, jnp.ones(v.shape, v.dtype)], axis=1)
    return jnp.dot(jnp.concatenate(rounded, axis=1), v, preferred_element_type=jnp.float32)


def near_kernel(
    slash_ref, base_ref, q_ref, far_ref, third_ref, second_ref, first_ref, own_ref, acc_ref, stat_ref, band, score_a, score_b, top_a, top_b, sems
):
    head = pl.program_id(0)
    slab_blocks = own_ref.shape[0]
    slash_count = slash_ref.shape[0] // pl.num_programs(0)

    @pl.when(head == 0)
    def _():
        start = 0
        copies = []
        for number, part in enumerate((far_ref, third_ref, second_ref, first_ref, own_ref)):
            copies.append(pltpu.make_async_copy(part, band.at[pl.ds(start, part.shape[0])], sems.at[number]))
            start += part.shape[0]
        for copy in copies:
            copy.start()
        for copy in copies:
            copy.wait()

    lanes = lax.broadcasted_iota(jnp.int32, (BLK, HD), 1)
    causal = lax.broadcasted_iota(jnp.int32, (BLK, BLK), 0) >= lanes
    base = base_ref[0]
    offsets = [slash_ref[head * slash_count + n] for n in range(slash_count)]
    buffers = ((score_a, top_a), (score_b, top_b))

    def places(index):
        return [index + REACH] + [index + REACH - s for s in offsets]

    def begin(index):
        flags = [True] + [base + index - s >= 0 for s in offsets]
        kts = [band[p, :BLK, :] for p in places(index)]
        score_stage(q_ref[index * BLK : (index + 1) * BLK, :], flags, kts, *buffers[index % 2], causal=causal)

    def finish(index):
        rows = slice(index * BLK, (index + 1) * BLK)
        score_ref, top_ref = buffers[index % 2]
        mixed = weight_stage(score_ref, top_ref, [band[p, BLK:, :] for p in places(index)])
        acc_ref[rows, :] = mixed[:, :HD]
        stat = jnp.where(lanes == 2 * head, top_ref[...], stat_ref[rows, :])
        stat_ref[rows, :] = jnp.where(lanes == 2 * head + 1, mixed[:, HD:], stat)

    begin(0)
    for index in range(slab_blocks):
        if index + 1 < slab_blocks:
            begin(index + 1)
        finish(index)


def near(slash, base, queries, far, third, second, first, own):
    rows, width = queries.shape
    heads = width // HD
    slab_blocks = rows // BLK
    slash_count = slash.shape[0] // heads
    hbm = pl.BlockSpec(memory_space=pl.ANY)
    return pl.pallas_call(
        near_kernel,
        grid_spec=pltpu.PrefetchScalarGridSpec(
            num_scalar_prefetch=2,
            grid=(heads,),
            in_specs=[pl.BlockSpec((rows, HD), lambda h, *_: (0, h))] + [hbm] * 5,
            out_specs=[
                pl.BlockSpec((rows, HD), lambda h, *_: (0, h)),
                pl.BlockSpec((rows, HD), lambda h, *_: (0, 0)),
            ],
            scratch_shapes=[
                pltpu.VMEM((REACH + slab_blocks, 2 * BLK, HD), jnp.bfloat16),
                pltpu.VMEM((BLK, (slash_count + 1) * BLK), jnp.float32),
                pltpu.VMEM((BLK, (slash_count + 1) * BLK), jnp.float32),
                pltpu.VMEM((BLK, HD), jnp.float32),
                pltpu.VMEM((BLK, HD), jnp.float32),
                pltpu.SemaphoreType.DMA((5,)),
            ],
        ),
        out_shape=[
            jax.ShapeDtypeStruct((rows, width), jnp.float32),
            jax.ShapeDtypeStruct((rows, HD), jnp.float32),
        ],
        compiler_params=pltpu.CompilerParams(dimension_semantics=("arbitrary",)),
        cost_estimate=cost(rows * heads * (slash_count + 1), rows * width * 8),
        name="near",
    )(slash, base, queries, far, third, second, first, own)


def vertical_kernel(slab_blocks, count, slot_ref, ok_ref, quarters_ref, *refs):
    ins, refs = refs[:6], refs[6:]
    columns, refs = refs[:count], refs[count:]
    outs, (score_a, score_b, top_a, top_b) = refs[:2], refs[2:]
    head = pl.program_id(0)
    blocks = outs[0].shape[0] // BLK
    lanes = lax.broadcasted_iota(jnp.int32, (BLK, HD), 1)
    kts = [c[0, :BLK, :] for c in columns]
    vs = [c[0, BLK:, :] for c in columns]
    buffers = ((score_a, top_a), (score_b, top_b))
    work = [(part, block) for part in range(2) for block in range(blocks)]

    def near_stat(part, block, which):
        stat = ins[3 * part + 2][block * BLK : (block + 1) * BLK, :]
        return jnp.sum(jnp.where(lanes == 2 * head + which, stat, 0.0), axis=1, keepdims=True)

    def begin(number):
        part, block = work[number]
        first = (head * slab_blocks + quarters_ref[part] * blocks + block) * count
        flags = [ok_ref[first + k] > 0 for k in range(count)]
        q = ins[3 * part][block * BLK : (block + 1) * BLK, :]
        score_stage(q, flags, kts, *buffers[number % 2], floor=near_stat(part, block, 0))

    def finish(number):
        part, block = work[number]
        rows = slice(block * BLK, (block + 1) * BLK)
        score_ref, top_ref = buffers[number % 2]
        mixed = weight_stage(score_ref, top_ref, vs)
        shrink = jnp.exp2(near_stat(part, block, 0) - top_ref[...])
        total = mixed[:, HD:] + near_stat(part, block, 1) * shrink
        whole = mixed[:, :HD] + ins[3 * part + 1][rows, :] * shrink
        outs[part][rows, :] = (whole / total).astype(outs[part].dtype)

    begin(0)
    for number in range(len(work)):
        if number + 1 < len(work):
            begin(number + 1)
        finish(number)


def vertical_half(slots, ok, quarters, queries, acc, stat, gathered, parts):
    rows, width = queries.shape
    heads = width // HD
    count = slots.shape[0] // heads
    part = rows // parts

    def column(k):
        return pl.BlockSpec((1, 2 * BLK, HD), lambda h, slot, ok, quarters: (slot[h * count + k], 0, 0))

    def own(which, fixed=False):
        return pl.BlockSpec((part, HD), lambda h, slot, ok, quarters: (quarters[which], 0 if fixed else h))

    return pl.pallas_call(
        functools.partial(vertical_kernel, rows // BLK, count),
        grid_spec=pltpu.PrefetchScalarGridSpec(
            num_scalar_prefetch=3,
            grid=(heads,),
            in_specs=[own(0), own(0), own(0, True), own(1), own(1), own(1, True)] + [column(k) for k in range(count)],
            out_specs=[pl.BlockSpec((part, HD), lambda h, *_: (0, h))] * 2,
            scratch_shapes=[
                pltpu.VMEM((BLK, count * BLK), jnp.float32),
                pltpu.VMEM((BLK, count * BLK), jnp.float32),
                pltpu.VMEM((BLK, HD), jnp.float32),
                pltpu.VMEM((BLK, HD), jnp.float32),
            ],
        ),
        out_shape=[jax.ShapeDtypeStruct((part, width), jnp.bfloat16)] * 2,
        compiler_params=pltpu.CompilerParams(dimension_semantics=("arbitrary",)),
        cost_estimate=cost(2 * part * heads * count, part * width * 32),
        name="vertical",
    )(slots, ok, quarters, *([queries, acc, stat] * 2), *([gathered] * count))


def tables(vertical, slash, slab_index, slab_blocks, row):
    blocks = jnp.arange(lax.axis_size(SEQ) * slab_blocks, dtype=jnp.int32)
    flat = vertical.reshape(-1)
    used = jnp.any(flat[:, None] == blocks[None, :], axis=0)
    earlier = (blocks[None, :] // slab_blocks == flat[:, None] // slab_blocks) & (blocks[None, :] < flat[:, None])
    rank = jnp.sum((earlier & used[None, :]).astype(jnp.int32), axis=1)
    slots = (flat // slab_blocks ^ row) * CAP + rank
    mine = slab_index * slab_blocks + jnp.arange(slab_blocks, dtype=jnp.int32)
    gap = mine[None, :, None] - vertical[:, None, :]
    covered = jnp.any(gap[..., None] == slash[:, None, None, :], axis=3)
    ok = (gap > 0) & jnp.logical_not(covered)
    return slots, ok.astype(jnp.int32).reshape(-1)


def shards(queries, keys, values, vertical, slash):
    slab_blocks = queries.shape[0] // BLK
    parts = lax.axis_size("head")
    slab_index = lax.axis_index(SEQ).astype(jnp.int32)
    base = (slab_index * slab_blocks).reshape(1)
    kv, packed = prep(vertical.reshape(-1), base, keys, values)
    slabs = lax.axis_size(SEQ)
    pair = lax.axis_size("y")

    def swapped(array):
        return lax.ppermute(array, "y", [(i, pair - 1 - i) for i in range(pair)])

    def from_before(array):
        return lax.ppermute(array, SEQ, [(i, (i + pair) % slabs) for i in range(slabs)])

    gathered = lax.all_gather(jnp.stack([packed, swapped(packed)]), ("x", "z"), axis=0, tiled=True)
    gathered = gathered.reshape(-1, *packed.shape[1:])
    upper = lax.axis_index("y") == 1
    second = from_before(kv)
    fourth = from_before(second)
    first = swapped(jnp.where(upper, second, kv))
    third = swapped(jnp.where(upper, fourth, second))
    far = fourth[slab_blocks - REACH % slab_blocks :]
    slots, ok = tables(vertical, slash, slab_index, slab_blocks, lax.axis_index("y").astype(jnp.int32))
    acc, stat = near(slash.reshape(-1), base, queries, far, third, second, first, kv)
    here = lax.axis_index("head").astype(jnp.int32)

    def half(pair):
        quarters = jnp.stack([here ^ step for step in pair])
        return vertical_half(slots, ok, quarters, queries, acc, stat, gathered, parts)

    def sent(piece, step):
        return lax.ppermute(piece, "head", [(i, i ^ step) for i in range(parts)])

    second_piece, third_piece = half((2, 3))
    first_piece, own_piece = half((1, 0))
    pieces = [own_piece, sent(first_piece, 1), sent(second_piece, 2), sent(third_piece, 3)]
    width = queries.shape[1]
    out = jnp.zeros((pieces[0].shape[0], width * parts), pieces[0].dtype)
    for step in (0, 1, 2, 3):
        out = lax.dynamic_update_slice_in_dim(out, pieces[step], (here ^ step) * width, 1)
    return out


def solution(mesh):
    split = Mesh(mesh.devices.reshape(mesh.shape["head"], 4, 4, 2), ("head",) + SEQ)
    return jax.shard_map(
        shards,
        mesh=split,
        in_specs=(P(SEQ, "head"), P(SEQ, "head"), P(SEQ, "head"), P("head", None), P("head", None)),
        out_specs=P(SEQ + ("head",), None),
        check_vma=False,
    )
```

profile of v0, /device:TPU:1, one launch (start us, length us, event | category | flops | bytes accessed | tf_op | source)
XLA Modules:
  0.0 164.8 jit_solution(13926253017549910913)
XLA Ops:
  6.5 1.4 reshape.129.flat_ref
  7.9 3.3 %prep.1 = (bf16[8,256,128]{2,1,0:T(8,128)(2,1)}, bf16[4,256,128]{2,1,0:T(8,128)(2,1)}) custom-call(s32[64]{0:T(128)} %reshape.129.flat_ref, s32[1]{0:T(128)} %bitcast.2.base_ref, bf16[1024,128]{1,0:T(8,128)(2,1)} %keys_ref.1, bf16[1024,128]{1,0:T(8,128)(2,1)} %values_ref.1), custom_call_target="tpu_custom_call" | custom-call | tf_op jit(solution)/shard_map/prep/pallas_call | solution.py:53
  11.2 2.1 %collective-permute-start.4 = (bf16[4,256,128]{2,1,0:T(8,128)(2,1)}, bf16[4,256,128]{2,1,0:T(8,128)(2,1)S(1)}, u32[]{:S(2)}, u32[]{:S(2)}) collective-permute-start(bf16[4,256,128]{2,1,0:T(8,128)(2,1)} %get-tuple-element.16), channel_id=1, source_target_pairs={{0,1},{1,0},{2,3},{3,2},{4,5},{5,4},{6,7},{7,6},{8,9},{9,8},{10,11... | collective-permute-start | bytes 786440 | tf_op jit(solution)/shard_map/ppermute | solution.py:289
  13.3 5.9 %collective-permute-done.4 = bf16[4,256,128]{2,1,0:T(8,128)(2,1)S(1)} collective-permute-done((bf16[4,256,128]{2,1,0:T(8,128)(2,1)}, bf16[4,256,128]{2,1,0:T(8,128)(2,1)S(1)}, u32[]{:S(2)}, u32[]{:S(2)}) %collective-permute-start.4) | collective-permute-done | bytes 262176 | tf_op jit(solution)/shard_map/ppermute | solution.py:289
  19.2 1.8 %pad_maximum_fusion = bf16[2,4,256,128]{3,2,1,0:T(8,128)(2,1)} fusion(bf16[1,4,256,128]{3,2,1,0:T(8,128)(2,1)S(1)} %bitcast.25, bf16[1,4,256,128]{3,2,1,0:T(8,128)(2,1)} %bitcast.24), kind=kLoop, calls=%fused_computation | loop fusion | flops 262144 | bytes 1048576 | tf_op jit(solution)/shard_map/stack | solution.py:294
  21.0 1.9 %collective-permute-start = (bf16[8,256,128]{2,1,0:T(8,128)(2,1)}, bf16[8,256,128]{2,1,0:T(8,128)(2,1)S(1)}, u32[]{:S(2)}, u32[]{:S(2)}) collective-permute-start(bf16[8,256,128]{2,1,0:T(8,128)(2,1)} %get-tuple-element.13.own_ref), channel_id=1, source_target_pairs={{0,2},{1,3},{2,4},{3,5},{4,6},{5,7},{6,8},{7,9},{8,10},{9,11},{10,... | collective-permute-start | bytes 1572872 | tf_op jit(solution)/shard_map/ppermute | solution.py:292
  23.0 0.6 reshape.130.slash_ref
  23.6 1.3 compare_reduce_fusion
  24.9 13.4 %collective-permute-done.second_ref = bf16[8,256,128]{2,1,0:T(8,128)(2,1)S(1)} collective-permute-done((bf16[8,256,128]{2,1,0:T(8,128)(2,1)}, bf16[8,256,128]{2,1,0:T(8,128)(2,1)S(1)}, u32[]{:S(2)}, u32[]{:S(2)}) %collective-permute-start) | collective-permute-done | bytes 524320 | tf_op jit(solution)/shard_map/ppermute | solution.py:292
  38.4 0.6 reshape.133.ok_ref
  39.0 0.6 pad_add_fusion
  39.6 0.1 fusion.2
  39.7 20.4 %collective-permute-done.1 = bf16[8,256,128]{2,1,0:T(8,128)(2,1)S(1)} collective-permute-done((bf16[8,256,128]{2,1,0:T(8,128)(2,1)S(1)}, bf16[8,256,128]{2,1,0:T(8,128)(2,1)S(1)}, u32[]{:S(2)}, u32[]{:S(2)}) %collective-permute-start.1) | collective-permute-done | bytes 524320 | tf_op jit(solution)/shard_map/ppermute | solution.py:292
  60.1 0.1 broadcast_select_fusion
  60.2 1.2 collective-permute-start.2
  61.4 0.3 collective-permute-start.3
  61.8 0.2 convert_reduce_fusion
  61.9 0.6 multiply_add_fusion.slot_ref
  62.5 0.7 slice.4.far_ref
  63.2 9.4 %collective-permute-done.2.third_ref = bf16[8,256,128]{2,1,0:T(8,128)(2,1)S(1)} collective-permute-done((bf16[8,256,128]{2,1,0:T(8,128)(2,1)S(1)}, bf16[8,256,128]{2,1,0:T(8,128)(2,1)S(1)}, u32[]{:S(2)}, u32[]{:S(2)}) %collective-permute-start.2) | collective-permute-done | bytes 524320 | tf_op jit(solution)/shard_map/ppermute | solution.py:289
  72.6 11.2 %collective-permute-done.3.first_ref = bf16[8,256,128]{2,1,0:T(8,128)(2,1)S(1)} collective-permute-done((bf16[8,256,128]{2,1,0:T(8,128)(2,1)S(1)}, bf16[8,256,128]{2,1,0:T(8,128)(2,1)S(1)}, u32[]{:S(2)}, u32[]{:S(2)}) %collective-permute-start.3) | collective-permute-done | bytes 524320 | tf_op jit(solution)/shard_map/ppermute | solution.py:289
  83.8 0.8 copy-done.8
  84.6 19.4 %near.1 = (f32[1024,1024]{1,0:T(8,128)}, f32[1024,128]{1,0:T(8,128)}) custom-call(s32[64]{0:T(128)} %reshape.130.slash_ref, s32[1]{0:T(128)} %bitcast.2.base_ref, bf16[1024,1024]{1,0:T(8,128)(2,1)} %refs_3_.3, bf16[4,256,128]{2,1,0:T(8,128)(2,1)} %slice.4.far_ref, bf16[8,256,128]{2,1,0:T(8,128)(2,1)} %copy-done.7, bf16[8,256,128]{2,1,0:T(8,128)(2,1)} %copy-done.3, ...), custom_call_target="tpu_custom_call" | custom-call | flops 4831838208 | bytes 8388608 | tf_op jit(solution)/shard_map/near/pallas_call | solution.py:163
  104.1 12.1 %vertical.2 = (bf16[256,1024]{1,0:T(8,128)(2,1)}, bf16[256,1024]{1,0:T(8,128)(2,1)}) custom-call(s32[64]{0:T(128)} %multiply_add_fusion.slot_ref, s32[512]{0:T(512)} %reshape.133.ok_ref, s32[2]{0:T(128)} %get-tuple-element.23.quarters_ref, bf16[1024,1024]{1,0:T(8,128)(2,1)} %refs_3_.3, f32[1024,1024]{1,0:T(8,128)} %get-tuple-element.14.refs_1_.refs_4_, ...), custom_call_target="tpu_custom_call" | custom-call | flops 2147483648 | bytes 8388608 | tf_op jit(solution)/shard_map/vertical/pallas_call | solution.py:244
  116.2 2.1 %collective-permute-start.5 = (bf16[256,1024]{1,0:T(8,128)(2,1)}, bf16[256,1024]{1,0:T(8,128)(2,1)S(1)}, u32[]{:S(2)}, u32[]{:S(2)}) collective-permute-start(bf16[256,1024]{1,0:T(8,128)(2,1)} %get-tuple-element.18), channel_id=1, source_target_pairs={{0,32},{32,0},{64,96},{96,64},{1,33},{33,1},{65,97},{97,65},{2,34}... | collective-permute-start | bytes 1572872 | tf_op jit(solution)/shard_map/ppermute | solution.py:311
  118.3 12.1 %vertical.3 = (bf16[256,1024]{1,0:T(8,128)(2,1)}, bf16[256,1024]{1,0:T(8,128)(2,1)}) custom-call(s32[64]{0:T(128)} %multiply_add_fusion.slot_ref, s32[512]{0:T(512)} %reshape.133.ok_ref, s32[2]{0:T(128)} %get-tuple-element.24.quarters_ref, bf16[1024,1024]{1,0:T(8,128)(2,1)} %refs_3_.3, f32[1024,1024]{1,0:T(8,128)} %get-tuple-element.14.refs_1_.refs_4_, ...), custom_call_target="tpu_custom_call" | custom-call | flops 2147483648 | bytes 8388608 | tf_op jit(solution)/shard_map/vertical/pallas_call | solution.py:244
  130.4 2.8 %collective-permute-start.6 = (bf16[256,1024]{1,0:T(8,128)(2,1)}, bf16[256,1024]{1,0:T(8,128)(2,1)S(1)}, u32[]{:S(2)}, u32[]{:S(2)}) collective-permute-start(bf16[256,1024]{1,0:T(8,128)(2,1)} %get-tuple-element.19), channel_id=1, source_target_pairs={{0,64},{32,96},{64,0},{96,32},{1,65},{33,97},{65,1},{97,33},{2,66}... | collective-permute-start | bytes 1572872 | tf_op jit(solution)/shard_map/ppermute | solution.py:311
  133.2 0.5 collective-permute-start.7
  133.6 0.2 broadcast_in_dim.2
  134.0 11.6 %collective-permute-done.6 = bf16[256,1024]{1,0:T(8,128)(2,1)S(1)} collective-permute-done((bf16[256,1024]{1,0:T(8,128)(2,1)}, bf16[256,1024]{1,0:T(8,128)(2,1)S(1)}, u32[]{:S(2)}, u32[]{:S(2)}) %collective-permute-start.6) | collective-permute-done | bytes 524320 | tf_op jit(solution)/shard_map/ppermute | solution.py:311
  145.7 11.4 %collective-permute-done.7 = bf16[256,1024]{1,0:T(8,128)(2,1)S(1)} collective-permute-done((bf16[256,1024]{1,0:T(8,128)(2,1)}, bf16[256,1024]{1,0:T(8,128)(2,1)S(1)}, u32[]{:S(2)}, u32[]{:S(2)}) %collective-permute-start.7) | collective-permute-done | bytes 524320 | tf_op jit(solution)/shard_map/ppermute | solution.py:311
  157.1 0.8 constant_dynamic-update-slice_fusion
  (30 shorter events, 0.4 us)
Async XLA Ops:
  6.5 17.0 %copy-start.4 = (s32[8,8]{1,0:T(8,128)S(1)}, s32[8,8]{1,0:T(8,128)}, u32[]{:S(2)}) copy-start(s32[8,8]{1,0:T(8,128)} %param.8) | copy-start | bytes 772
  6.5 16.4 %copy-start.5 = (s32[8,8]{1,0:T(8,128)S(1)}, s32[8,8]{1,0:T(8,128)}, u32[]{:S(2)}) copy-start(s32[8,8]{1,0:T(8,128)} %param.9) | copy-start | bytes 772
  6.5 97.6 %all-gather.2.cloned.1.call-start = ((), (), s32[]{:S(2)}) async-start(), calls=%async_computation | async-start | bytes 8912896 | tf_op jit(solution)/shard_map/all_gather | solution.py:294
  7.9 31.7 %copy-start.6 = (s32[64]{0:T(128)S(1)}, s32[64]{0:T(128)}, u32[]{:S(2)}) copy-start(s32[64]{0:T(128)} %reshape.129.flat_ref) | copy-start | bytes 772
  11.2 48.9 %copy-start.2 = (bf16[8,256,128]{2,1,0:T(8,128)(2,1)S(1)}, bf16[8,256,128]{2,1,0:T(8,128)(2,1)}, u32[]{:S(2)}) copy-start(bf16[8,256,128]{2,1,0:T(8,128)(2,1)} %get-tuple-element.13.own_ref) | copy-start | bytes 1572868
  11.2 8.0 %collective-permute-start.4 = (bf16[4,256,128]{2,1,0:T(8,128)(2,1)}, bf16[4,256,128]{2,1,0:T(8,128)(2,1)S(1)}, u32[]{:S(2)}, u32[]{:S(2)}) collective-permute-start(bf16[4,256,128]{2,1,0:T(8,128)(2,1)} %get-tuple-element.16), channel_id=1, source_target_pairs={{0,1},{1,0},{2,3},{3,2},{4,5},{5,4},{6,7},{7,6},{8,9},{9,8},{10,11... | collective-permute-start | bytes 786440 | tf_op jit(solution)/shard_map/ppermute | solution.py:289
  21.0 17.3 %collective-permute-start = (bf16[8,256,128]{2,1,0:T(8,128)(2,1)}, bf16[8,256,128]{2,1,0:T(8,128)(2,1)S(1)}, u32[]{:S(2)}, u32[]{:S(2)}) collective-permute-start(bf16[8,256,128]{2,1,0:T(8,128)(2,1)} %get-tuple-element.13.own_ref), channel_id=1, source_target_pairs={{0,2},{1,3},{2,4},{3,5},{4,6},{5,7},{6,8},{7,9},{8,10},{9,11},{10,... | collective-permute-start | bytes 1572872 | tf_op jit(solution)/shard_map/ppermute | solution.py:292
  38.3 45.6 %copy-start.3 = (bf16[8,256,128]{2,1,0:T(8,128)(2,1)}, bf16[8,256,128]{2,1,0:T(8,128)(2,1)S(1)}, u32[]{:S(2)}) copy-start(bf16[8,256,128]{2,1,0:T(8,128)(2,1)S(1)} %collective-permute-done.second_ref) | copy-start | bytes 1572868
  38.3 21.8 %collective-permute-start.1 = (bf16[8,256,128]{2,1,0:T(8,128)(2,1)S(1)}, bf16[8,256,128]{2,1,0:T(8,128)(2,1)S(1)}, u32[]{:S(2)}, u32[]{:S(2)}) collective-permute-start(bf16[8,256,128]{2,1,0:T(8,128)(2,1)S(1)} %collective-permute-done.second_ref), channel_id=1, source_target_pairs={{0,2},{1,3},{2,4},{3,5},{4,6},{5,7},{6,8},{7,9},{8,10},{9,11},{10,... | collective-permute-start | bytes 1572872 | tf_op jit(solution)/shard_map/ppermute | solution.py:292
  60.2 12.4 %collective-permute-start.2 = (bf16[8,256,128]{2,1,0:T(8,128)(2,1)S(1)}, bf16[8,256,128]{2,1,0:T(8,128)(2,1)S(1)}, u32[]{:S(2)}, u32[]{:S(2)}) collective-permute-start(bf16[8,256,128]{2,1,0:T(8,128)(2,1)S(1)} %get-tuple-element.22), channel_id=1, source_target_pairs={{0,1},{1,0},{2,3},{3,2},{4,5},{5,4},{6,7},{7,6},{8,9},{9,8},{10,11... | collective-permute-start | bytes 1572872 | tf_op jit(solution)/shard_map/ppermute | solution.py:289
  61.4 22.4 %collective-permute-start.3 = (bf16[8,256,128]{2,1,0:T(8,128)(2,1)S(1)}, bf16[8,256,128]{2,1,0:T(8,128)(2,1)S(1)}, u32[]{:S(2)}, u32[]{:S(2)}) collective-permute-start(bf16[8,256,128]{2,1,0:T(8,128)(2,1)S(1)} %get-tuple-element.21), channel_id=1, source_target_pairs={{0,1},{1,0},{2,3},{3,2},{4,5},{5,4},{6,7},{7,6},{8,9},{9,8},{10,11... | collective-permute-start | bytes 1572872 | tf_op jit(solution)/shard_map/ppermute | solution.py:289
  72.6 11.2 %copy-start.7 = (bf16[8,256,128]{2,1,0:T(8,128)(2,1)}, bf16[8,256,128]{2,1,0:T(8,128)(2,1)S(1)}, u32[]{:S(2)}) copy-start(bf16[8,256,128]{2,1,0:T(8,128)(2,1)S(1)} %collective-permute-done.2.third_ref) | copy-start | bytes 1572868
  83.8 0.8 copy-start.8
  116.2 17.7 %collective-permute-start.5 = (bf16[256,1024]{1,0:T(8,128)(2,1)}, bf16[256,1024]{1,0:T(8,128)(2,1)S(1)}, u32[]{:S(2)}, u32[]{:S(2)}) collective-permute-start(bf16[256,1024]{1,0:T(8,128)(2,1)} %get-tuple-element.18), channel_id=1, source_target_pairs={{0,32},{32,0},{64,96},{96,64},{1,33},{33,1},{65,97},{97,65},{2,34}... | collective-permute-start | bytes 1572872 | tf_op jit(solution)/shard_map/ppermute | solution.py:311
  130.4 3.5 %copy-start.1 = (bf16[256,1024]{1,0:T(8,128)(2,1)S(1)}, bf16[256,1024]{1,0:T(8,128)(2,1)}, u32[]{:S(2)}) copy-start(bf16[256,1024]{1,0:T(8,128)(2,1)} %get-tuple-element.17) | copy-start | bytes 1572868
  130.4 15.2 %collective-permute-start.6 = (bf16[256,1024]{1,0:T(8,128)(2,1)}, bf16[256,1024]{1,0:T(8,128)(2,1)S(1)}, u32[]{:S(2)}, u32[]{:S(2)}) collective-permute-start(bf16[256,1024]{1,0:T(8,128)(2,1)} %get-tuple-element.19), channel_id=1, source_target_pairs={{0,64},{32,96},{64,0},{96,32},{1,65},{33,97},{65,1},{97,33},{2,66}... | collective-permute-start | bytes 1572872 | tf_op jit(solution)/shard_map/ppermute | solution.py:311
  133.2 23.9 %collective-permute-start.7 = (bf16[256,1024]{1,0:T(8,128)(2,1)}, bf16[256,1024]{1,0:T(8,128)(2,1)S(1)}, u32[]{:S(2)}, u32[]{:S(2)}) collective-permute-start(bf16[256,1024]{1,0:T(8,128)(2,1)} %get-tuple-element.20), channel_id=1, source_target_pairs={{0,96},{32,64},{64,32},{96,0},{1,97},{33,65},{65,33},{97,1},{2,98}... | collective-permute-start | bytes 1572872 | tf_op jit(solution)/shard_map/ppermute | solution.py:311
  145.7 11.4 %copy-start = (bf16[256,4096]{1,0:T(8,128)(2,1)}, bf16[256,4096]{1,0:T(8,128)(2,1)S(1)}, u32[]{:S(2)}) copy-start(bf16[256,4096]{1,0:T(8,128)(2,1)S(1)} %constant_dynamic-update-slice_fusion.1) | copy-start | bytes 6291460
Sparse Core Ops, SparseCore 0:
  21.1 82.0 all-gather.1
where the time goes:
time: 165 us
  waiting for transfers between devices  83.3 us (50%)
  Pallas kernels  46.9 us (28%)
  between operations  13.5 us (8%)
  starting transfers between devices  10.9 us (7%)
  local copies, waits for them, and re-layouts  5.31 us (3%)
  other arithmetic  4.79 us (3%)
    ppermute x2, waiting for transfers between devices, from_before(): lax.ppermute(array, SEQ, [(i, (i + pair) % slabs) for i in range(slabs)])  33.8 us
    ppermute x3, waiting for transfers between devices, swapped(): return lax.ppermute(array, 'y', [(i, pair - 1 - i) for i in range(pair)])  26.5 us
    pallas_call x2, Pallas kernels, vertical_half(): pl.pallas_call(functools.partial(vertical_kernel, rows // BLK, count), gr...  24.2 us
    ppermute x3, waiting for transfers between devices, sent(): return lax.ppermute(piece, 'head', [(i, i ^ step) for i in range(parts)])  23 us
    pallas_call x1, Pallas kernels, near(): pl.pallas_call(near_kernel, grid_spec=pltpu.PrefetchScalarGridSpec(num_sc...  19.4 us
    ppermute x3, starting transfers between devices, sent(): return lax.ppermute(piece, 'head', [(i, i ^ step) for i in range(parts)])  5.32 us
    ppermute x3, starting transfers between devices, swapped(): return lax.ppermute(array, 'y', [(i, pair - 1 - i) for i in range(pair)])  3.66 us
  transfers between devices with their start and end apart: 9, of which 7 were waited for; matrix products, arithmetic and copies ran while one was open for 3% of the time, Pallas kernels for 19%

commit v1 on v0

v1 whole, which is shorter than its diff:
```python
import functools
import math

import jax
import jax.numpy as jnp
from jax import lax
from jax.experimental import pallas as pl
from jax.experimental.pallas import tpu as pltpu
from jax.sharding import Mesh
from jax.sharding import PartitionSpec as P

BLK = 128
HD = 128
REACH = 28
CAP = 4
NEG = -1e30
SEQ = ("x", "z", "y")
SCALE2 = math.log2(math.e) / math.sqrt(HD)


def cost(row_blocks, moved):
    return pl.CostEstimate(flops=row_blocks * 4 * BLK * HD, bytes_accessed=moved, transcendentals=row_blocks * BLK)


def prep_kernel(vertical_ref, base_ref, keys_ref, values_ref, kv_ref, packed_ref):
    slab_blocks = kv_ref.shape[0]
    base = base_ref[0]

    bits = jnp.int32(0)
    for head in range(vertical_ref.shape[0]):
        for number in range(vertical_ref.shape[1]):
            local = vertical_ref[head, number] - base
            inside = (local >= 0) & (local < slab_blocks)
            bits = bits | jnp.where(inside, 1 << jnp.where(inside, local, 0), 0)
    packed_ref[...] = jnp.zeros(packed_ref.shape, packed_ref.dtype)
    rank = jnp.int32(0)
    for block in range(slab_blocks):
        rows = pl.ds(block * BLK, BLK)
        kv_ref[block, :BLK, :] = keys_ref[rows, :].T
        kv_ref[block, BLK:, :] = values_ref[rows, :]
        used = (bits >> block) & 1

        @pl.when((used == 1) & (rank < CAP))
        def _(block=block, rank=rank):
            packed_ref[rank] = kv_ref[block]

        rank = rank + used


def prep(vertical, base, keys, values):
    slab_blocks = keys.shape[0] // BLK
    whole = lambda shape: pl.BlockSpec(shape, lambda *_: (0,) * len(shape))
    return pl.pallas_call(
        prep_kernel,
        grid_spec=pltpu.PrefetchScalarGridSpec(
            num_scalar_prefetch=2,
            grid=(1,),
            in_specs=[whole(keys.shape), whole(values.shape)],
            out_specs=[whole((slab_blocks, 2 * BLK, HD)), whole((CAP, 2 * BLK, HD))],
        ),
        out_shape=[
            jax.ShapeDtypeStruct((slab_blocks, 2 * BLK, HD), jnp.bfloat16),
            jax.ShapeDtypeStruct((CAP, 2 * BLK, HD), jnp.bfloat16),
        ],
        name="prep",
    )(vertical, base, keys, values)


def bias_columns(flags, rows):
    lanes = lax.broadcasted_iota(jnp.int32, (8, HD), 1)
    columns = jnp.zeros((8, HD), jnp.float32)
    for n, flag in enumerate(flags):
        columns = jnp.where(lanes == n, jnp.where(flag, 0.0, NEG).astype(jnp.float32), columns)
    return jnp.broadcast_to(columns[:1], (rows, HD)).astype(jnp.bfloat16)


def marker_rows(n):
    return (lax.broadcasted_iota(jnp.int32, (HD, BLK), 0) == n).astype(jnp.bfloat16)


def score_stage(q, flags, kts, score_ref, top_ref, causal=None, floor=None):
    left = jnp.concatenate([q, bias_columns(flags, q.shape[0])], axis=1)
    right = jnp.concatenate(
        [jnp.concatenate([kt, marker_rows(n)], axis=0) for n, kt in enumerate(kts)], axis=1
    )
    scores = jnp.dot(left, right, preferred_element_type=jnp.float32)
    parts = [scores[:, n * BLK : (n + 1) * BLK] * SCALE2 for n in range(len(kts))]
    if causal is not None:
        parts[0] = jnp.where(causal, parts[0], NEG)
    for n, part in enumerate(parts):
        score_ref[:, n * BLK : (n + 1) * BLK] = part
    top = jnp.max(functools.reduce(jnp.maximum, parts), axis=1, keepdims=True)
    if floor is not None:
        top = jnp.maximum(top, floor)
    top_ref[...] = jnp.broadcast_to(top, top_ref.shape)


def weight_stage(score_ref, top_ref, vs):
    top = top_ref[...]
    rounded = []
    for n in range(len(vs)):
        weights = jnp.exp2(score_ref[:, n * BLK : (n + 1) * BLK] - top)
        rounded.append(weights.astype(jnp.bfloat16))
    v = jnp.concatenate(vs, axis=0)
    v = jnp.concatenate([v, jnp.ones(v.shape, v.dtype)], axis=1)
    return jnp.dot(jnp.concatenate(rounded, axis=1), v, preferred_element_type=jnp.float32)


def near_kernel(
    slash_ref, base_ref, q_ref, next_q_ref, far_ref, third_ref, second_ref, first_ref, own_ref, near_ref, stat_ref, band, score_a, score_b, top_a, top_b, sems
):
    head = pl.program_id(0)
    heads = pl.num_programs(0)
    slab_blocks = own_ref.shape[0]
    slash_count = slash_ref.shape[1]
    lanes = lax.broadcasted_iota(jnp.int32, (BLK, HD), 1)
    causal = lax.broadcasted_iota(jnp.int32, (BLK, BLK), 0) >= lanes
    base = base_ref[0]
    buffers = ((score_a, top_a), (score_b, top_b))

    def offsets_of(which):
        return [slash_ref[which, n] for n in range(slash_count)]

    def places(index, offsets):
        return [index + REACH] + [index + REACH - s for s in offsets]

    def begin(q, index, offsets):
        flags = [True] + [base + index - s >= 0 for s in offsets]
        kts = [band[p, :BLK, :] for p in places(index, offsets)]
        score_stage(q[index * BLK : (index + 1) * BLK, :], flags, kts, *buffers[index % 2], causal=causal)

    def finish(index, offsets):
        rows = slice(index * BLK, (index + 1) * BLK)
        score_ref, top_ref = buffers[index % 2]
        mixed = weight_stage(score_ref, top_ref, [band[p, BLK:, :] for p in places(index, offsets)])
        total = mixed[:, HD:]
        near_ref[rows, :] = mixed[:, :HD] / total
        stat_ref[rows, :] = jnp.where(lanes == head, top_ref[...] + jnp.log2(total), stat_ref[rows, :])

    offsets = offsets_of(head)
    following = offsets_of(jnp.minimum(head + 1, heads - 1))

    @pl.when(head == 0)
    def _():
        start = 0
        copies = []
        for number, part in enumerate((far_ref, third_ref, second_ref, first_ref, own_ref)):
            copies.append(pltpu.make_async_copy(part, band.at[pl.ds(start, part.shape[0])], sems.at[number]))
            start += part.shape[0]
        for copy in copies:
            copy.start()
        for copy in copies:
            copy.wait()
        begin(q_ref, 0, offsets)

    for index in range(slab_blocks):
        if index + 1 < slab_blocks:
            begin(q_ref, index + 1, offsets)
        else:
            begin(next_q_ref, 0, following)
        finish(index, offsets)


def near(slash, base, queries, far, third, second, first, own):
    rows, width = queries.shape
    heads = width // HD
    slab_blocks = rows // BLK
    slash_count = slash.shape[1]
    assert slab_blocks % 2 == 0
    hbm = pl.BlockSpec(memory_space=pl.ANY)
    return pl.pallas_call(
        near_kernel,
        grid_spec=pltpu.PrefetchScalarGridSpec(
            num_scalar_prefetch=2,
            grid=(heads,),
            in_specs=[
                pl.BlockSpec((rows, HD), lambda h, *_: (0, h)),
                pl.BlockSpec((BLK, HD), lambda h, *_: (0, jnp.minimum(h + 1, heads - 1))),
            ]
            + [hbm] * 5,
            out_specs=[
                pl.BlockSpec((rows, HD), lambda h, *_: (0, h)),
                pl.BlockSpec((rows, HD), lambda h, *_: (0, 0)),
            ],
            scratch_shapes=[
                pltpu.VMEM((REACH + slab_blocks, 2 * BLK, HD), jnp.bfloat16),
                pltpu.VMEM((BLK, (slash_count + 1) * BLK), jnp.float32),
                pltpu.VMEM((BLK, (slash_count + 1) * BLK), jnp.float32),
                pltpu.VMEM((BLK, HD), jnp.float32),
                pltpu.VMEM((BLK, HD), jnp.float32),
                pltpu.SemaphoreType.DMA((5,)),
            ],
        ),
        out_shape=[
            jax.ShapeDtypeStruct((rows, width), jnp.float32),
            jax.ShapeDtypeStruct((rows, HD), jnp.float32),
        ],
        compiler_params=pltpu.CompilerParams(dimension_semantics=("arbitrary",)),
        cost_estimate=cost(rows * heads * (slash_count + 1), rows * width * 8),
        name="near",
    )(slash, base, queries, queries, far, third, second, first, own)


def vertical_kernel(count, slot_ref, ok_ref, quarters_ref, *refs):
    ins, refs = refs[:8], refs[8:]
    colours, refs = (refs[:5], refs[5:10]), refs[10:]
    outs, (columns, score_a, score_b, top_a, top_b, stat_a, stat_b, sems) = refs[:2], refs[2:]
    step = pl.program_id(0)
    heads = 2 * pl.num_programs(0)
    depth = columns.shape[0]
    piece = colours[0][0].shape[0]
    part_rows = outs[0].shape[0]
    blocks = part_rows // BLK
    lanes = lax.broadcasted_iota(jnp.int32, (2 * part_rows, HD), 1)
    buffers = ((score_a, top_a, stat_a), (score_b, top_b, stat_b))

    def fetch(which):
        place = which % depth
        for k in range(count):
            slot = slot_ref[which * count + k]
            colour, region, inner = slot // (4 * piece), slot // piece % 4, slot % piece
            half = piece // 2
            for number, (own, ahead, low, high, behind) in enumerate(colours):

                @pl.when(colour == number)
                def _(own=own, ahead=ahead, low=low, high=high, behind=behind, k=k, region=region, inner=inner):
                    def take(condition, source, index):
                        @pl.when(condition)
                        def _():
                            pltpu.make_async_copy(source.at[index], columns.at[place, k], sems.at[place]).start()

                    take(region == 0, own, inner)
                    take(region == 1, ahead, inner)
                    take((region == 2) & (inner < half), low, inner)
                    take((region == 2) & (inner >= half), high, inner - half)
                    take(region == 3, behind, inner)

    def arrive(which):
        place = which % depth
        pltpu.make_async_copy(columns.at[place], columns.at[place], sems.at[place]).wait()

    def guarded(action, which):
        @pl.when(which < heads)
        def _():
            action(which)

    def begin(which, qs, buffer):
        score_ref, top_ref, stat_ref = buffer
        biases = []
        for part in range(2):
            for block in range(blocks):
                here = quarters_ref[part] * blocks + block
                flags = [ok_ref[which, here * count + k] > 0 for k in range(count)]
                biases.append(bias_columns(flags, BLK))
        left = jnp.concatenate([jnp.concatenate(qs, axis=0), jnp.concatenate(biases, axis=0)], axis=1)
        stat = jnp.concatenate([ins[3][...], ins[7][...]], axis=0)
        top = jnp.sum(jnp.where(lanes == which, stat, 0.0), axis=1, keepdims=True)
        stat_ref[...] = jnp.broadcast_to(top, stat_ref.shape)
        tops = []
        for k in range(0, count, 2):
            pair = [
                jnp.concatenate([columns[which % depth, n, :BLK], marker_rows(n)], axis=0) for n in (k, k + 1)
            ]
            scores = jnp.dot(left, jnp.concatenate(pair, axis=1), preferred_element_type=jnp.float32) * SCALE2
            score_ref[:, k * BLK : (k + 2) * BLK] = scores
            tops.append(jnp.maximum(scores[:, :BLK], scores[:, BLK:]))
        top = jnp.maximum(top, jnp.max(functools.reduce(jnp.maximum, tops), axis=1, keepdims=True))
        top_ref[...] = jnp.broadcast_to(top, top_ref.shape)

    def finish(which, local, buffer):
        score_ref, top_ref, stat_ref = buffer
        mixed = weight_stage(score_ref, top_ref, [columns[which % depth, k, BLK:] for k in range(count)])
        weight = jnp.exp2(stat_ref[...] - top_ref[...])
        near_part = jnp.concatenate([ins[2][:, local], ins[6][:, local]], axis=0)
        whole = (mixed[:, :HD] + near_part * weight) / (mixed[:, HD:] + weight)
        for part in range(2):
            outs[part][:, local] = whole[part * part_rows : (part + 1) * part_rows].astype(outs[part].dtype)

    first, second = slice(0, HD), slice(HD, 2 * HD)

    @pl.when(step == 0)
    def _():
        for which in range(3):
            fetch(which)
        arrive(0)
        begin(0, [ins[0][:, first], ins[4][:, first]], buffers[0])

    for offset in (1, 2):
        guarded(arrive, 2 * step + offset)
    for offset in (3, 4):
        guarded(fetch, 2 * step + offset)
    begin(2 * step + 1, [ins[0][:, second], ins[4][:, second]], buffers[1])
    finish(2 * step, first, buffers[0])
    begin(jnp.minimum(2 * step + 2, heads - 1), [ins[1][...], ins[5][...]], buffers[0])
    finish(2 * step + 1, second, buffers[1])


def vertical_half(slots, ok, quarters, queries, near_part, stat, last_z, last_x):
    rows, width = queries.shape
    heads = width // HD
    count = slots.shape[0] // heads
    part = rows // 4
    assert heads % 2 == 0 and heads > 2 and count % 2 == 0
    hbm = pl.BlockSpec(memory_space=pl.ANY)

    def own(which, lanes, column):
        return pl.BlockSpec((part, lanes), lambda t, slot, ok, quarters: (quarters[which], column(t)))

    def mine(which):
        return [
            own(which, 2 * HD, lambda t: t),
            own(which, HD, lambda t: jnp.minimum(2 * t + 2, heads - 1)),
            own(which, 2 * HD, lambda t: t),
            own(which, HD, lambda t: 0),
        ]

    return pl.pallas_call(
        functools.partial(vertical_kernel, count),
        grid_spec=pltpu.PrefetchScalarGridSpec(
            num_scalar_prefetch=3,
            grid=(heads // 2,),
            in_specs=mine(0) + mine(1) + [hbm] * 10,
            out_specs=[pl.BlockSpec((part, 2 * HD), lambda t, *_: (0, t))] * 2,
            scratch_shapes=[pltpu.VMEM((6, count, 2 * BLK, HD), jnp.bfloat16)]
            + [pltpu.VMEM((2 * part, count * BLK), jnp.float32)] * 2
            + [pltpu.VMEM((2 * part, HD), jnp.float32)] * 4
            + [pltpu.SemaphoreType.DMA((6,))],
        ),
        out_shape=[jax.ShapeDtypeStruct((part, width), jnp.bfloat16)] * 2,
        compiler_params=pltpu.CompilerParams(dimension_semantics=("arbitrary",)),
        cost_estimate=cost(2 * part * heads * count, part * width * 32),
        name="vertical",
    )(slots, ok, quarters, *([queries, queries, near_part, stat] * 2), *last_z, *last_x)


def tables(vertical, slash, slab_index, slab_blocks):
    heads, _ = vertical.shape
    blocks = jnp.arange(lax.axis_size(SEQ) * slab_blocks, dtype=jnp.int32)
    flat = vertical.reshape(-1)
    used = jnp.any(flat[:, None] == blocks[None, :], axis=0)
    earlier = (blocks[None, :] // slab_blocks == flat[:, None] // slab_blocks) & (blocks[None, :] < flat[:, None])
    rank = jnp.sum((earlier & used[None, :]).astype(jnp.int32), axis=1)
    slab = flat // slab_blocks
    xs, zs, ys = lax.axis_size("x"), lax.axis_size("z"), lax.axis_size("y")
    dx = (slab // (zs * ys) - lax.axis_index("x")) % xs
    dz = (slab // ys - lax.axis_index("z")) % zs
    half = CAP // 2
    last_x = rank >= half
    piece = jnp.where(last_x, xs * zs + dx * zs + dz, dz * xs + dx)
    slots = (piece * ys + (slab % ys ^ lax.axis_index("y"))) * half + rank % half
    mine = slab_index * slab_blocks + jnp.arange(slab_blocks, dtype=jnp.int32)
    gap = mine[None, :, None] - vertical[:, None, :]
    covered = jnp.any(gap[..., None] == slash[:, None, None, :], axis=3)
    ok = (gap > 0) & jnp.logical_not(covered)
    return slots, ok.astype(jnp.int32).reshape(heads, -1)


def from_ahead(array, axis, by):
    size = lax.axis_size(axis)
    return lax.ppermute(array, axis, [((i + by) % size, i) for i in range(size)])


def along(array, axis):
    return jnp.concatenate([array] + [from_ahead(array, axis, by) for by in (1, 2, 3)], axis=0)


def around(array, axis):
    half = array.shape[0] // 2
    ahead, behind = from_ahead(array, axis, 1), from_ahead(array, axis, 3)
    low, high = from_ahead(ahead[:half], axis, 1), from_ahead(behind[half:], axis, 3)
    return [array, ahead, low, high, behind]


def step(queries, keys, values, vertical, slash):
    slab_blocks = queries.shape[0] // BLK
    parts = lax.axis_size("head")
    slab_index = lax.axis_index(SEQ).astype(jnp.int32)
    base = (slab_index * slab_blocks).reshape(1)
    kv, packed = prep(vertical, base, keys, values)
    slabs = lax.axis_size(SEQ)
    pair = lax.axis_size("y")

    def swapped(array):
        return lax.ppermute(array, "y", [(i, pair - 1 - i) for i in range(pair)])

    def from_before(array, pairs):
        return lax.ppermute(array, SEQ, [(i, (i + pairs * pair) % slabs) for i in range(slabs)])

    half = CAP // 2
    other = swapped(packed)
    last_z = around(along(jnp.concatenate([packed[:half], other[:half]], axis=0), "x"), "z")
    last_x = around(along(jnp.concatenate([packed[half:], other[half:]], axis=0), "z"), "x")
    upper = lax.axis_index("y") == 1
    second, fourth = from_before(kv, 1), from_before(kv, 2)
    first = swapped(jnp.where(upper, second, kv))
    third = swapped(jnp.where(upper, *lax.optimization_barrier((fourth, second))))
    far = fourth[slab_blocks - REACH % slab_blocks :]
    slots, ok = tables(vertical, slash, slab_index, slab_blocks)
    near_part, stat = near(slash, base, queries, far, third, second, first, kv)
    here = lax.axis_index("head").astype(jnp.int32)

    def half(pair):
        quarters = jnp.stack([here ^ step for step in pair])
        return vertical_half(slots, ok, quarters, queries, near_part, stat, last_z, last_x)

    def sent(piece, step):
        return lax.ppermute(piece, "head", [(i, i ^ step) for i in range(parts)])

    second_piece, third_piece = half((2, 3))
    first_piece, own_piece = half((1, 0))
    pieces = [own_piece, sent(first_piece, 1), sent(second_piece, 2), sent(third_piece, 3)]
    width = queries.shape[1]
    out = jnp.zeros((pieces[0].shape[0], width * parts), pieces[0].dtype)
    for step in (0, 1, 2, 3):
        out = lax.dynamic_update_slice_in_dim(out, pieces[step], (here ^ step) * width, 1)
    return out


def solution(mesh):
    split = Mesh(mesh.devices.reshape(mesh.shape["head"], 4, 4, 2), ("head",) + SEQ)
    return jax.shard_map(
        step,
        mesh=split,
        in_specs=(P(SEQ, "head"), P(SEQ, "head"), P(SEQ, "head"), P("head", None), P("head", None)),
        out_specs=P(SEQ + ("head",), None),
        check_vma=False,
    )
```

time: 165 us -> 162 us (0.982)
  the two profiles are of different devices: /device:TPU:1 before, /device:TPU:2 now
where the time goes in v1:
time: 162 us; the launch traced here: 160 us
  waiting for transfers between devices  54.4 us (34%)
  Pallas kernels  45.9 us (28%)
  starting transfers between devices  37.5 us (23%)
  local copies, waits for them, and re-layouts  15.4 us (10%)
  other arithmetic  6.4 us (4%)
    ppermute x14, waiting for transfers between devices, from_ahead(): lax.ppermute(array, axis, [((i + by) % size, i) for i in range(size)])  28.6 us
    ppermute x14, starting transfers between devices, from_ahead(): lax.ppermute(array, axis, [((i + by) % size, i) for i in range(size)])  23.7 us
    pallas_call x2, Pallas kernels, vertical_half(): pl.pallas_call(functools.partial(vertical_kernel, count), grid_spec=pltpu...  23.2 us
    ppermute x3, waiting for transfers between devices, sent(): return lax.ppermute(piece, 'head', [(i, i ^ step) for i in range(parts)])  23 us
    pallas_call x1, Pallas kernels, near(): pl.pallas_call(near_kernel, grid_spec=pltpu.PrefetchScalarGridSpec(num_sc...  19.3 us
    ppermute x2, starting transfers between devices, from_before(): lax.ppermute(array, SEQ, [(i, (i + pairs * pair) % slabs) for i in range(...  5.52 us
    ppermute x3, starting transfers between devices, swapped(): return lax.ppermute(array, 'y', [(i, pair - 1 - i) for i in range(pair)])  4.69 us
    unnamed x24, local copies, waits for them, and re-layouts  4.11 us
  transfers between devices with their start and end apart: 22, of which 10 were waited for; matrix products, arithmetic and copies ran while one was open for 12% of the time, Pallas kernels for 19%

profile of v1, /device:TPU:2, one launch (start us, length us, event | category | flops | bytes accessed | tf_op | source)
XLA Modules:
  0.0 160.0 jit_solution(9368315672742219455)
XLA Ops:
  0.0 3.5 %prep.1 = (bf16[8,256,128]{2,1,0:T(8,128)(2,1)}, bf16[4,256,128]{2,1,0:T(8,128)(2,1)}) custom-call(s32[8,8]{1,0:T(8,128)} %vertical_ref.1, s32[1]{0:T(128)} %bitcast.2.base_ref, bf16[1024,128]{1,0:T(8,128)(2,1)} %keys_ref.1, bf16[1024,128]{1,0:T(8,128)(2,1)} %values_ref.1), custom_call_target="tpu_custom_call" | custom-call | tf_op jit(solution)/shard_map/prep/pallas_call | solution.py:53
  3.5 1.9 %collective-permute-start.1 = (bf16[8,256,128]{2,1,0:T(8,128)(2,1)}, bf16[8,256,128]{2,1,0:T(8,128)(2,1)}, u32[]{:S(2)}, u32[]{:S(2)}) collective-permute-start(bf16[8,256,128]{2,1,0:T(8,128)(2,1)} %get-tuple-element.15.own_ref), channel_id=1, source_target_pairs={{0,2},{1,3},{2,4},{3,5},{4,6},{5,7},{6,8},{7,9},{8,10},{9,11},{10,... | collective-permute-start | bytes 1572872 | tf_op jit(solution)/shard_map/ppermute | solution.py:387
  5.4 3.6 %collective-permute-start = (bf16[8,256,128]{2,1,0:T(8,128)(2,1)}, bf16[8,256,128]{2,1,0:T(8,128)(2,1)}, u32[]{:S(2)}, u32[]{:S(2)}) collective-permute-start(bf16[8,256,128]{2,1,0:T(8,128)(2,1)} %get-tuple-element.15.own_ref), channel_id=1, source_target_pairs={{0,4},{1,5},{2,6},{3,7},{4,8},{5,9},{6,10},{7,11},{8,12},{9,13},{1... | collective-permute-start | bytes 1572872 | tf_op jit(solution)/shard_map/ppermute | solution.py:387
  9.0 1.6 collective-permute-start.4
  12.1 1.7 %fusion.12 = (bf16[2,256,128]{2,1,0:T(8,128)(2,1)S(1)}, bf16[16,256,128]{2,1,0:T(8,128)(2,1)}, bf16[16,256,128]{2,1,0:T(8,128)(2,1)}, bf16[2,256,128]{2,1,0:T(8,128)(2,1)S(1)}) fusion(bf16[4,256,128]{2,1,0:T(8,128)(2,1)} %get-tuple-element.20), kind=kLoop, calls=%fused_computation.65 | loop fusion | bytes 786432 | tf_op jit(solution)/shard_map/slice | solution.py:392
  13.8 2.8 %collective-permute-done.4 = bf16[4,256,128]{2,1,0:T(8,128)(2,1)S(1)} collective-permute-done((bf16[4,256,128]{2,1,0:T(8,128)(2,1)}, bf16[4,256,128]{2,1,0:T(8,128)(2,1)S(1)}, u32[]{:S(2)}, u32[]{:S(2)}) %collective-permute-start.4) | collective-permute-done | bytes 262176 | tf_op jit(solution)/shard_map/ppermute | solution.py:384
  17.5 2.0 %collective-permute-start.12 = (bf16[4,256,128]{2,1,0:T(8,128)(2,1)S(1)}, bf16[4,256,128]{2,1,0:T(8,128)(2,1)S(1)}, u32[]{:S(2)}, u32[]{:S(2)}) collective-permute-start(bf16[4,256,128]{2,1,0:T(8,128)(2,1)S(1)} %pad_maximum_fusion.1), channel_id=1, source_target_pairs={{2,0},{4,2},{6,4},{0,6},{3,1},{5,3},{7,5},{1,7},{10,8},{12,10},{14... | collective-permute-start | bytes 786440 | tf_op jit(solution)/shard_map/ppermute | solution.py:360
  19.5 1.3 compare_reduce_fusion
  21.9 5.2 %collective-permute-done.12 = bf16[4,256,128]{2,1,0:T(8,128)(2,1)S(1)} collective-permute-done((bf16[4,256,128]{2,1,0:T(8,128)(2,1)S(1)}, bf16[4,256,128]{2,1,0:T(8,128)(2,1)S(1)}, u32[]{:S(2)}, u32[]{:S(2)}) %collective-permute-start.12) | collective-permute-done | bytes 262176 | tf_op jit(solution)/shard_map/ppermute | solution.py:360
  28.4 10.0 %collective-permute-done.13 = bf16[4,256,128]{2,1,0:T(8,128)(2,1)S(1)} collective-permute-done((bf16[4,256,128]{2,1,0:T(8,128)(2,1)S(1)}, bf16[4,256,128]{2,1,0:T(8,128)(2,1)S(1)}, u32[]{:S(2)}, u32[]{:S(2)}) %collective-permute-start.13) | collective-permute-done | bytes 262176 | tf_op jit(solution)/shard_map/ppermute | solution.py:360
  38.3 2.1 %collective-permute-start.6 = (bf16[4,256,128]{2,1,0:T(8,128)(2,1)S(1)}, bf16[4,256,128]{2,1,0:T(8,128)(2,1)S(1)}, u32[]{:S(2)}, u32[]{:S(2)}) collective-permute-start(bf16[4,256,128]{2,1,0:T(8,128)(2,1)S(1)} %pad_maximum_fusion), channel_id=1, source_target_pairs={{16,0},{24,8},{0,16},{8,24},{17,1},{25,9},{1,17},{9,25},{18,2},{26... | collective-permute-start | bytes 786440 | tf_op jit(solution)/shard_map/ppermute | solution.py:360
  42.1 1.6 %collective-permute-start.7 = (bf16[4,256,128]{2,1,0:T(8,128)(2,1)S(1)}, bf16[4,256,128]{2,1,0:T(8,128)(2,1)S(1)}, u32[]{:S(2)}, u32[]{:S(2)}) collective-permute-start(bf16[4,256,128]{2,1,0:T(8,128)(2,1)S(1)} %pad_maximum_fusion), channel_id=1, source_target_pairs={{24,0},{0,8},{8,16},{16,24},{25,1},{1,9},{9,17},{17,25},{26,2},{2,... | collective-permute-start | bytes 786440 | tf_op jit(solution)/shard_map/ppermute | solution.py:360
  44.4 1.1 collective-permute-start.15
  46.9 2.6 %collective-permute-start.17 = (bf16[16,256,128]{2,1,0:T(8,128)(2,1)}, bf16[16,256,128]{2,1,0:T(8,128)(2,1)S(1)}, u32[]{:S(2)}, u32[]{:S(2)}) collective-permute-start(bf16[16,256,128]{2,1,0:T(8,128)(2,1)} %constant_dynamic-update-slice_fusion.5.refs_13_), channel_id=1, source_target_pairs={{24,0},{0,8},{8,16},{16,24},{25,1},{1,9},{9,17},{17,25},{26,2},{2,... | collective-permute-start | bytes 3145736 | tf_op jit(solution)/shard_map/ppermute | solution.py:360
  50.2 3.4 %collective-permute-done.7 = bf16[4,256,128]{2,1,0:T(8,128)(2,1)S(1)} collective-permute-done((bf16[4,256,128]{2,1,0:T(8,128)(2,1)S(1)}, bf16[4,256,128]{2,1,0:T(8,128)(2,1)S(1)}, u32[]{:S(2)}, u32[]{:S(2)}) %collective-permute-start.7) | collective-permute-done | bytes 262176 | tf_op jit(solution)/shard_map/ppermute | solution.py:360
  54.3 4.2 %collective-permute-start.10 = (bf16[16,256,128]{2,1,0:T(8,128)(2,1)}, bf16[16,256,128]{2,1,0:T(8,128)(2,1)S(1)}, u32[]{:S(2)}, u32[]{:S(2)}) collective-permute-start(bf16[16,256,128]{2,1,0:T(8,128)(2,1)} %constant_dynamic-update-slice_fusion.refs_8_), channel_id=1, source_target_pairs={{6,0},{0,2},{2,4},{4,6},{7,1},{1,3},{3,5},{5,7},{14,8},{8,10},{10,... | collective-permute-start | bytes 3145736 | tf_op jit(solution)/shard_map/ppermute | solution.py:360
  58.7 1.1 broadcast_select_fusion.1
  59.8 1.6 collective-permute-start.2
  61.4 1.1 broadcast_select_fusion
  62.5 6.8 %collective-permute-done.15.refs_14_ = bf16[16,256,128]{2,1,0:T(8,128)(2,1)S(1)} collective-permute-done((bf16[16,256,128]{2,1,0:T(8,128)(2,1)}, bf16[16,256,128]{2,1,0:T(8,128)(2,1)S(1)}, u32[]{:S(2)}, u32[]{:S(2)}) %collective-permute-start.15) | collective-permute-done | bytes 1048608 | tf_op jit(solution)/shard_map/ppermute | solution.py:360
  69.3 1.6 collective-permute-start.3
  72.9 2.1 %collective-permute-done.17.refs_17_ = bf16[16,256,128]{2,1,0:T(8,128)(2,1)S(1)} collective-permute-done((bf16[16,256,128]{2,1,0:T(8,128)(2,1)}, bf16[16,256,128]{2,1,0:T(8,128)(2,1)S(1)}, u32[]{:S(2)}, u32[]{:S(2)}) %collective-permute-start.17) | collective-permute-done | bytes 1048608 | tf_op jit(solution)/shard_map/ppermute | solution.py:360
  74.9 3.0 %collective-permute-start.16 = (bf16[8,256,128]{2,1,0:T(8,128)(2,1)}, bf16[8,256,128]{2,1,0:T(8,128)(2,1)}, u32[]{:S(2)}, u32[]{:S(2)}) collective-permute-start(bf16[8,256,128]{2,1,0:T(8,128)(2,1)} %slice.41), channel_id=1, source_target_pairs={{8,0},{16,8},{24,16},{0,24},{9,1},{17,9},{25,17},{1,25},{10,2},{18... | collective-permute-start | bytes 1572872 | tf_op jit(solution)/shard_map/ppermute | solution.py:360
  78.8 2.4 %collective-permute-start.18 = (bf16[8,256,128]{2,1,0:T(8,128)(2,1)}, bf16[8,256,128]{2,1,0:T(8,128)(2,1)}, u32[]{:S(2)}, u32[]{:S(2)}) collective-permute-start(bf16[8,256,128]{2,1,0:T(8,128)(2,1)} %slice.42), channel_id=1, source_target_pairs={{24,0},{0,8},{8,16},{16,24},{25,1},{1,9},{9,17},{17,25},{26,2},{2,... | collective-permute-start | bytes 1572872 | tf_op jit(solution)/shard_map/ppermute | solution.py:360
  83.3 3.1 %collective-permute-start.9 = (bf16[8,256,128]{2,1,0:T(8,128)(2,1)}, bf16[8,256,128]{2,1,0:T(8,128)(2,1)S(1)}, u32[]{:S(2)}, u32[]{:S(2)}) collective-permute-start(bf16[8,256,128]{2,1,0:T(8,128)(2,1)} %slice.38), channel_id=1, source_target_pairs={{2,0},{4,2},{6,4},{0,6},{3,1},{5,3},{7,5},{1,7},{10,8},{12,10},{14... | collective-permute-start | bytes 1572872 | tf_op jit(solution)/shard_map/ppermute | solution.py:360
  87.0 1.7 %slice.36.far_ref = bf16[4,256,128]{2,1,0:T(8,128)(2,1)} slice(bf16[8,256,128]{2,1,0:T(8,128)(2,1)} %collective-permute-done), slice={[4:8], [0:256], [0:128]} | slice | bytes 524288 | tf_op jit(solution)/shard_map/slice | solution.py:397
  88.7 19.3 %near.1 = (f32[1024,1024]{1,0:T(8,128)}, f32[1024,128]{1,0:T(8,128)}) custom-call(s32[8,8]{1,0:T(8,128)} %slash_ref.1, s32[1]{0:T(128)} %bitcast.2.base_ref, bf16[1024,1024]{1,0:T(8,128)(2,1)} %refs_5_.3, bf16[1024,1024]{1,0:T(8,128)(2,1)} %refs_5_.3, bf16[4,256,128]{2,1,0:T(8,128)(2,1)} %slice.36.far_ref, bf16[8,256,128]{2,1,0:T(8,128)(2,1)} %copy-done.9, ...), custom_call_target="tpu_custom_call" | custom-call | flops 4831838208 | bytes 8388608 | tf_op jit(solution)/shard_map/near/pallas_call | solution.py:171
  108.9 11.6 %vertical.2 = (bf16[256,1024]{1,0:T(8,128)(2,1)}, bf16[256,1024]{1,0:T(8,128)(2,1)}) custom-call(s32[64]{0:T(128)} %fusion.5.slot_ref, s32[8,64]{1,0:T(8,128)} %fusion.4.ok_ref, s32[2]{0:T(128)} %get-tuple-element.33.quarters_ref, bf16[1024,1024]{1,0:T(8,128)(2,1)} %refs_5_.3, bf16[1024,1024]{1,0:T(8,128)(2,1)} %refs_5_.3, ...), custom_call_target="tpu_custom_call" | custom-call | flops 2147483648 | bytes 8388608 | tf_op jit(solution)/shard_map/vertical/pallas_call | solution.py:317
  120.6 11.6 %vertical.3 = (bf16[256,1024]{1,0:T(8,128)(2,1)}, bf16[256,1024]{1,0:T(8,128)(2,1)}) custom-call(s32[64]{0:T(128)} %fusion.5.slot_ref, s32[8,64]{1,0:T(8,128)} %fusion.4.ok_ref, s32[2]{0:T(128)} %get-tuple-element.34.quarters_ref, bf16[1024,1024]{1,0:T(8,128)(2,1)} %refs_5_.3, bf16[1024,1024]{1,0:T(8,128)(2,1)} %refs_5_.3, ...), custom_call_target="tpu_custom_call" | custom-call | flops 2147483648 | bytes 8388608 | tf_op jit(solution)/shard_map/vertical/pallas_call | solution.py:317
  132.2 3.4 %collective-permute-start.20 = (bf16[256,1024]{1,0:T(8,128)(2,1)}, bf16[256,1024]{1,0:T(8,128)(2,1)S(1)}, u32[]{:S(2)}, u32[]{:S(2)}) collective-permute-start(bf16[256,1024]{1,0:T(8,128)(2,1)} %get-tuple-element.23), channel_id=1, source_target_pairs={{0,64},{32,96},{64,0},{96,32},{1,65},{33,97},{65,1},{97,33},{2,66}... | collective-permute-start | bytes 1572872 | tf_op jit(solution)/shard_map/ppermute | solution.py:407
  136.1 12.7 %collective-permute-done.20 = bf16[256,1024]{1,0:T(8,128)(2,1)S(1)} collective-permute-done((bf16[256,1024]{1,0:T(8,128)(2,1)}, bf16[256,1024]{1,0:T(8,128)(2,1)S(1)}, u32[]{:S(2)}, u32[]{:S(2)}) %collective-permute-start.20) | collective-permute-done | bytes 524320 | tf_op jit(solution)/shard_map/ppermute | solution.py:407
  148.8 10.3 %collective-permute-done.21 = bf16[256,1024]{1,0:T(8,128)(2,1)S(1)} collective-permute-done((bf16[256,1024]{1,0:T(8,128)(2,1)}, bf16[256,1024]{1,0:T(8,128)(2,1)S(1)}, u32[]{:S(2)}, u32[]{:S(2)}) %collective-permute-start.21) | collective-permute-done | bytes 524320 | tf_op jit(solution)/shard_map/ppermute | solution.py:407
  (75 shorter events, 17.9 us)
Async XLA Ops:
  0.0 19.5 %copy-start.8 = (s32[8,8]{1,0:T(8,128)S(1)}, s32[8,8]{1,0:T(8,128)}, u32[]{:S(2)}) copy-start(s32[8,8]{1,0:T(8,128)} %slash_ref.1) | copy-start | bytes 772
  3.5 55.1 %collective-permute-start.1 = (bf16[8,256,128]{2,1,0:T(8,128)(2,1)}, bf16[8,256,128]{2,1,0:T(8,128)(2,1)}, u32[]{:S(2)}, u32[]{:S(2)}) collective-permute-start(bf16[8,256,128]{2,1,0:T(8,128)(2,1)} %get-tuple-element.15.own_ref), channel_id=1, source_target_pairs={{0,2},{1,3},{2,4},{3,5},{4,6},{5,7},{6,8},{7,9},{8,10},{9,11},{10,... | collective-permute-start | bytes 1572872 | tf_op jit(solution)/shard_map/ppermute | solution.py:387
  5.4 53.3 %collective-permute-start = (bf16[8,256,128]{2,1,0:T(8,128)(2,1)}, bf16[8,256,128]{2,1,0:T(8,128)(2,1)}, u32[]{:S(2)}, u32[]{:S(2)}) collective-permute-start(bf16[8,256,128]{2,1,0:T(8,128)(2,1)} %get-tuple-element.15.own_ref), channel_id=1, source_target_pairs={{0,4},{1,5},{2,6},{3,7},{4,8},{5,9},{6,10},{7,11},{8,12},{9,13},{1... | collective-permute-start | bytes 1572872 | tf_op jit(solution)/shard_map/ppermute | solution.py:387
  9.0 7.7 %collective-permute-start.4 = (bf16[4,256,128]{2,1,0:T(8,128)(2,1)}, bf16[4,256,128]{2,1,0:T(8,128)(2,1)S(1)}, u32[]{:S(2)}, u32[]{:S(2)}) collective-permute-start(bf16[4,256,128]{2,1,0:T(8,128)(2,1)} %get-tuple-element.20), channel_id=1, source_target_pairs={{0,1},{1,0},{2,3},{3,2},{4,5},{5,4},{6,7},{7,6},{8,9},{9,8},{10,11... | collective-permute-start | bytes 786440 | tf_op jit(solution)/shard_map/ppermute | solution.py:384
  12.1 33.7 %copy-start.7 = (s32[8,8]{1,0:T(8,128)S(1)}, s32[8,8]{1,0:T(8,128)}, u32[]{:S(2)}) copy-start(s32[8,8]{1,0:T(8,128)} %vertical_ref.1) | copy-start | bytes 772
  17.5 9.6 %collective-permute-start.12 = (bf16[4,256,128]{2,1,0:T(8,128)(2,1)S(1)}, bf16[4,256,128]{2,1,0:T(8,128)(2,1)S(1)}, u32[]{:S(2)}, u32[]{:S(2)}) collective-permute-start(bf16[4,256,128]{2,1,0:T(8,128)(2,1)S(1)} %pad_maximum_fusion.1), channel_id=1, source_target_pairs={{2,0},{4,2},{6,4},{0,6},{3,1},{5,3},{7,5},{1,7},{10,8},{12,10},{14... | collective-permute-start | bytes 786440 | tf_op jit(solution)/shard_map/ppermute | solution.py:360
  20.7 17.6 %collective-permute-start.13 = (bf16[4,256,128]{2,1,0:T(8,128)(2,1)S(1)}, bf16[4,256,128]{2,1,0:T(8,128)(2,1)S(1)}, u32[]{:S(2)}, u32[]{:S(2)}) collective-permute-start(bf16[4,256,128]{2,1,0:T(8,128)(2,1)S(1)} %pad_maximum_fusion.1), channel_id=1, source_target_pairs={{4,0},{6,2},{0,4},{2,6},{5,1},{7,3},{1,5},{3,7},{12,8},{14,10},{8,... | collective-permute-start | bytes 786440 | tf_op jit(solution)/shard_map/ppermute | solution.py:360
  20.9 21.1 %collective-permute-start.14 = (bf16[4,256,128]{2,1,0:T(8,128)(2,1)S(1)}, bf16[4,256,128]{2,1,0:T(8,128)(2,1)S(1)}, u32[]{:S(2)}, u32[]{:S(2)}) collective-permute-start(bf16[4,256,128]{2,1,0:T(8,128)(2,1)S(1)} %pad_maximum_fusion.1), channel_id=1, source_target_pairs={{6,0},{0,2},{2,4},{4,6},{7,1},{1,3},{3,5},{5,7},{14,8},{8,10},{10,... | collective-permute-start | bytes 786440 | tf_op jit(solution)/shard_map/ppermute | solution.py:360
  27.1 17.3 %collective-permute-start.5 = (bf16[4,256,128]{2,1,0:T(8,128)(2,1)S(1)}, bf16[4,256,128]{2,1,0:T(8,128)(2,1)S(1)}, u32[]{:S(2)}, u32[]{:S(2)}) collective-permute-start(bf16[4,256,128]{2,1,0:T(8,128)(2,1)S(1)} %pad_maximum_fusion), channel_id=1, source_target_pairs={{8,0},{16,8},{24,16},{0,24},{9,1},{17,9},{25,17},{1,25},{10,2},{18... | collective-permute-start | bytes 786440 | tf_op jit(solution)/shard_map/ppermute | solution.py:360
  38.3 8.5 %collective-permute-start.6 = (bf16[4,256,128]{2,1,0:T(8,128)(2,1)S(1)}, bf16[4,256,128]{2,1,0:T(8,128)(2,1)S(1)}, u32[]{:S(2)}, u32[]{:S(2)}) collective-permute-start(bf16[4,256,128]{2,1,0:T(8,128)(2,1)S(1)} %pad_maximum_fusion), channel_id=1, source_target_pairs={{16,0},{24,8},{0,16},{8,24},{17,1},{25,9},{1,17},{9,25},{18,2},{26... | collective-permute-start | bytes 786440 | tf_op jit(solution)/shard_map/ppermute | solution.py:360
  42.1 11.5 %collective-permute-start.7 = (bf16[4,256,128]{2,1,0:T(8,128)(2,1)S(1)}, bf16[4,256,128]{2,1,0:T(8,128)(2,1)S(1)}, u32[]{:S(2)}, u32[]{:S(2)}) collective-permute-start(bf16[4,256,128]{2,1,0:T(8,128)(2,1)S(1)} %pad_maximum_fusion), channel_id=1, source_target_pairs={{24,0},{0,8},{8,16},{16,24},{25,1},{1,9},{9,17},{17,25},{26,2},{2,... | collective-permute-start | bytes 786440 | tf_op jit(solution)/shard_map/ppermute | solution.py:360
  44.4 24.9 %collective-permute-start.15 = (bf16[16,256,128]{2,1,0:T(8,128)(2,1)}, bf16[16,256,128]{2,1,0:T(8,128)(2,1)S(1)}, u32[]{:S(2)}, u32[]{:S(2)}) collective-permute-start(bf16[16,256,128]{2,1,0:T(8,128)(2,1)} %constant_dynamic-update-slice_fusion.5.refs_13_), channel_id=1, source_target_pairs={{8,0},{16,8},{24,16},{0,24},{9,1},{17,9},{25,17},{1,25},{10,2},{18... | collective-permute-start | bytes 3145736 | tf_op jit(solution)/shard_map/ppermute | solution.py:360
  46.9 28.1 %collective-permute-start.17 = (bf16[16,256,128]{2,1,0:T(8,128)(2,1)}, bf16[16,256,128]{2,1,0:T(8,128)(2,1)S(1)}, u32[]{:S(2)}, u32[]{:S(2)}) collective-permute-start(bf16[16,256,128]{2,1,0:T(8,128)(2,1)} %constant_dynamic-update-slice_fusion.5.refs_13_), channel_id=1, source_target_pairs={{24,0},{0,8},{8,16},{16,24},{25,1},{1,9},{9,17},{17,25},{26,2},{2,... | collective-permute-start | bytes 3145736 | tf_op jit(solution)/shard_map/ppermute | solution.py:360
  54.3 24.4 %collective-permute-start.10 = (bf16[16,256,128]{2,1,0:T(8,128)(2,1)}, bf16[16,256,128]{2,1,0:T(8,128)(2,1)S(1)}, u32[]{:S(2)}, u32[]{:S(2)}) collective-permute-start(bf16[16,256,128]{2,1,0:T(8,128)(2,1)} %constant_dynamic-update-slice_fusion.refs_8_), channel_id=1, source_target_pairs={{6,0},{0,2},{2,4},{4,6},{7,1},{1,3},{3,5},{5,7},{14,8},{8,10},{10,... | collective-permute-start | bytes 3145736 | tf_op jit(solution)/shard_map/ppermute | solution.py:360
  58.5 23.5 %collective-permute-start.8 = (bf16[16,256,128]{2,1,0:T(8,128)(2,1)}, bf16[16,256,128]{2,1,0:T(8,128)(2,1)S(1)}, u32[]{:S(2)}, u32[]{:S(2)}) collective-permute-start(bf16[16,256,128]{2,1,0:T(8,128)(2,1)} %constant_dynamic-update-slice_fusion.refs_8_), channel_id=1, source_target_pairs={{2,0},{4,2},{6,4},{0,6},{3,1},{5,3},{7,5},{1,7},{10,8},{12,10},{14... | collective-permute-start | bytes 3145736 | tf_op jit(solution)/shard_map/ppermute | solution.py:360
  59.8 23.1 %collective-permute-start.2 = (bf16[8,256,128]{2,1,0:T(8,128)(2,1)S(1)}, bf16[8,256,128]{2,1,0:T(8,128)(2,1)S(1)}, u32[]{:S(2)}, u32[]{:S(2)}) collective-permute-start(bf16[8,256,128]{2,1,0:T(8,128)(2,1)S(1)} %broadcast_select_fusion.1), channel_id=1, source_target_pairs={{0,1},{1,0},{2,3},{3,2},{4,5},{5,4},{6,7},{7,6},{8,9},{9,8},{10,11... | collective-permute-start | bytes 1572872 | tf_op jit(solution)/shard_map/ppermute | solution.py:384
  69.3 13.6 %copy-start = (bf16[16,256,128]{2,1,0:T(8,128)(2,1)}, bf16[16,256,128]{2,1,0:T(8,128)(2,1)S(1)}, u32[]{:S(2)}) copy-start(bf16[16,256,128]{2,1,0:T(8,128)(2,1)S(1)} %collective-permute-done.15.refs_14_) | copy-start | bytes 3145732
  69.3 19.4 %collective-permute-start.3 = (bf16[8,256,128]{2,1,0:T(8,128)(2,1)S(1)}, bf16[8,256,128]{2,1,0:T(8,128)(2,1)}, u32[]{:S(2)}, u32[]{:S(2)}) collective-permute-start(bf16[8,256,128]{2,1,0:T(8,128)(2,1)S(1)} %broadcast_select_fusion), channel_id=1, source_target_pairs={{0,1},{1,0},{2,3},{3,2},{4,5},{5,4},{6,7},{7,6},{8,9},{9,8},{10,11... | collective-permute-start | bytes 1572872 | tf_op jit(solution)/shard_map/ppermute | solution.py:384
  74.9 33.1 %copy-start.1 = (bf16[16,256,128]{2,1,0:T(8,128)(2,1)}, bf16[16,256,128]{2,1,0:T(8,128)(2,1)S(1)}, u32[]{:S(2)}) copy-start(bf16[16,256,128]{2,1,0:T(8,128)(2,1)S(1)} %collective-permute-done.17.refs_17_) | copy-start | bytes 3145732
  74.9 33.1 %collective-permute-start.16 = (bf16[8,256,128]{2,1,0:T(8,128)(2,1)}, bf16[8,256,128]{2,1,0:T(8,128)(2,1)}, u32[]{:S(2)}, u32[]{:S(2)}) collective-permute-start(bf16[8,256,128]{2,1,0:T(8,128)(2,1)} %slice.41), channel_id=1, source_target_pairs={{8,0},{16,8},{24,16},{0,24},{9,1},{17,9},{25,17},{1,25},{10,2},{18... | collective-permute-start | bytes 1572872 | tf_op jit(solution)/shard_map/ppermute | solution.py:360
  78.8 29.3 %copy-start.2 = (bf16[16,256,128]{2,1,0:T(8,128)(2,1)}, bf16[16,256,128]{2,1,0:T(8,128)(2,1)S(1)}, u32[]{:S(2)}) copy-start(bf16[16,256,128]{2,1,0:T(8,128)(2,1)S(1)} %collective-permute-done.10.refs_12_) | copy-start | bytes 3145732
  78.8 29.3 %collective-permute-start.18 = (bf16[8,256,128]{2,1,0:T(8,128)(2,1)}, bf16[8,256,128]{2,1,0:T(8,128)(2,1)}, u32[]{:S(2)}, u32[]{:S(2)}) collective-permute-start(bf16[8,256,128]{2,1,0:T(8,128)(2,1)} %slice.42), channel_id=1, source_target_pairs={{24,0},{0,8},{8,16},{16,24},{25,1},{1,9},{9,17},{17,25},{26,2},{2,... | collective-permute-start | bytes 1572872 | tf_op jit(solution)/shard_map/ppermute | solution.py:360
  82.0 1.3 copy-start.3
  82.0 26.1 %collective-permute-start.11 = (bf16[8,256,128]{2,1,0:T(8,128)(2,1)}, bf16[8,256,128]{2,1,0:T(8,128)(2,1)}, u32[]{:S(2)}, u32[]{:S(2)}) collective-permute-start(bf16[8,256,128]{2,1,0:T(8,128)(2,1)} %slice.39), channel_id=1, source_target_pairs={{6,0},{0,2},{2,4},{4,6},{7,1},{1,3},{3,5},{5,7},{14,8},{8,10},{10,... | collective-permute-start | bytes 1572872 | tf_op jit(solution)/shard_map/ppermute | solution.py:360
  83.3 3.1 %copy-start.9 = (bf16[8,256,128]{2,1,0:T(8,128)(2,1)}, bf16[8,256,128]{2,1,0:T(8,128)(2,1)S(1)}, u32[]{:S(2)}) copy-start(bf16[8,256,128]{2,1,0:T(8,128)(2,1)S(1)} %collective-permute-done.2.third_ref) | copy-start | bytes 1572868
  83.3 24.8 %collective-permute-start.9 = (bf16[8,256,128]{2,1,0:T(8,128)(2,1)}, bf16[8,256,128]{2,1,0:T(8,128)(2,1)S(1)}, u32[]{:S(2)}, u32[]{:S(2)}) collective-permute-start(bf16[8,256,128]{2,1,0:T(8,128)(2,1)} %slice.38), channel_id=1, source_target_pairs={{2,0},{4,2},{6,4},{0,6},{3,1},{5,3},{7,5},{1,7},{10,8},{12,10},{14... | collective-permute-start | bytes 1572872 | tf_op jit(solution)/shard_map/ppermute | solution.py:360
  108.1 0.8 copy-start.4
  120.5 15.5 %collective-permute-start.19 = (bf16[256,1024]{1,0:T(8,128)(2,1)}, bf16[256,1024]{1,0:T(8,128)(2,1)S(1)}, u32[]{:S(2)}, u32[]{:S(2)}) collective-permute-start(bf16[256,1024]{1,0:T(8,128)(2,1)} %get-tuple-element.22), channel_id=1, source_target_pairs={{0,32},{32,0},{64,96},{96,64},{1,33},{33,1},{65,97},{97,65},{2,34}... | collective-permute-start | bytes 1572872 | tf_op jit(solution)/shard_map/ppermute | solution.py:407
  132.2 3.8 %copy-start.6 = (bf16[256,1024]{1,0:T(8,128)(2,1)S(1)}, bf16[256,1024]{1,0:T(8,128)(2,1)}, u32[]{:S(2)}) copy-start(bf16[256,1024]{1,0:T(8,128)(2,1)} %get-tuple-element.21) | copy-start | bytes 1572868
  132.2 16.6 %collective-permute-start.20 = (bf16[256,1024]{1,0:T(8,128)(2,1)}, bf16[256,1024]{1,0:T(8,128)(2,1)S(1)}, u32[]{:S(2)}, u32[]{:S(2)}) collective-permute-start(bf16[256,1024]{1,0:T(8,128)(2,1)} %get-tuple-element.23), channel_id=1, source_target_pairs={{0,64},{32,96},{64,0},{96,32},{1,65},{33,97},{65,1},{97,33},{2,66}... | collective-permute-start | bytes 1572872 | tf_op jit(solution)/shard_map/ppermute | solution.py:407
  135.6 23.5 %collective-permute-start.21 = (bf16[256,1024]{1,0:T(8,128)(2,1)}, bf16[256,1024]{1,0:T(8,128)(2,1)S(1)}, u32[]{:S(2)}, u32[]{:S(2)}) collective-permute-start(bf16[256,1024]{1,0:T(8,128)(2,1)} %get-tuple-element.24), channel_id=1, source_target_pairs={{0,96},{32,64},{64,32},{96,0},{1,97},{33,65},{65,33},{97,1},{2,98}... | collective-permute-start | bytes 1572872 | tf_op jit(solution)/shard_map/ppermute | solution.py:407
  148.8 10.3 %copy-start.5 = (bf16[256,4096]{1,0:T(8,128)(2,1)}, bf16[256,4096]{1,0:T(8,128)(2,1)S(1)}, u32[]{:S(2)}) copy-start(bf16[256,4096]{1,0:T(8,128)(2,1)S(1)} %constant_dynamic-update-slice_fusion.11) | copy-start | bytes 6291460

commit v2 on v1

--- a/solution.py
+++ b/solution.py
@@ -106,11 +106,10 @@
     return jnp.dot(jnp.concatenate(rounded, axis=1), v, preferred_element_type=jnp.float32)
 
 
-def near_kernel(
-    slash_ref, base_ref, q_ref, next_q_ref, far_ref, third_ref, second_ref, first_ref, own_ref, near_ref, stat_ref, band, score_a, score_b, top_a, top_b, sems
-):
-    head = pl.program_id(0)
-    heads = pl.num_programs(0)
+def near_kernel(first_head, slash_ref, base_ref, q_ref, next_q_ref, far_ref, third_ref, second_ref, first_ref, own_ref, *refs):
+    near_ref, stat_ref, band, score_a, score_b, top_a, top_b, sems = refs[-8:]
+    head = first_head + pl.program_id(0)
+    last_head = first_head + pl.num_programs(0) - 1
     slab_blocks = own_ref.shape[0]
     slash_count = slash_ref.shape[1]
     lanes = lax.broadcasted_iota(jnp.int32, (BLK, HD), 1)
@@ -138,13 +137,16 @@
         stat_ref[rows, :] = jnp.where(lanes == head, top_ref[...] + jnp.log2(total), stat_ref[rows, :])
 
     offsets = offsets_of(head)
-    following = offsets_of(jnp.minimum(head + 1, heads - 1))
-
-    @pl.when(head == 0)
+    following = offsets_of(jnp.minimum(head + 1, last_head))
+
+    @pl.when(head == first_head)
     def _():
+        if first_head:
+            stat_ref[...] = refs[1][...]
         start = 0
         copies = []
-        for number, part in enumerate((far_ref, third_ref, second_ref, first_ref, own_ref)):
+        far = far_ref.at[pl.ds(slab_blocks - REACH % slab_blocks, REACH % slab_blocks)]
+        for number, part in enumerate((far, third_ref, second_ref, first_ref, own_ref)):
             copies.append(pltpu.make_async_copy(part, band.at[pl.ds(start, part.shape[0])], sems.at[number]))
             start += part.shape[0]
         for copy in copies:
@@ -161,25 +163,26 @@
         finish(index, offsets)
 
 
-def near(slash, base, queries, far, third, second, first, own):
+def near(slash, base, queries, fourth, third, second, first, own, heads, done=()):
     rows, width = queries.shape
-    heads = width // HD
+    first_head = heads.start
     slab_blocks = rows // BLK
     slash_count = slash.shape[1]
     assert slab_blocks % 2 == 0
     hbm = pl.BlockSpec(memory_space=pl.ANY)
     return pl.pallas_call(
-        near_kernel,
+        functools.partial(near_kernel, first_head),
         grid_spec=pltpu.PrefetchScalarGridSpec(
             num_scalar_prefetch=2,
-            grid=(heads,),
+            grid=(len(heads),),
             in_specs=[
-                pl.BlockSpec((rows, HD), lambda h, *_: (0, h)),
-                pl.BlockSpec((BLK, HD), lambda h, *_: (0, jnp.minimum(h + 1, heads - 1))),
+                pl.BlockSpec((rows, HD), lambda h, *_: (0, first_head + h)),
+                pl.BlockSpec((BLK, HD), lambda h, *_: (0, jnp.minimum(first_head + h + 1, heads.stop - 1))),
             ]
-            + [hbm] * 5,
+            + [hbm] * 5
+            + [hbm, pl.BlockSpec((rows, HD), lambda h, *_: (0, 0))][: len(done)],
             out_specs=[
-                pl.BlockSpec((rows, HD), lambda h, *_: (0, h)),
+                pl.BlockSpec((rows, HD), lambda h, *_: (0, first_head + h)),
                 pl.BlockSpec((rows, HD), lambda h, *_: (0, 0)),
             ],
             scratch_shapes=[
@@ -196,44 +199,51 @@
             jax.ShapeDtypeStruct((rows, HD), jnp.float32),
         ],
         compiler_params=pltpu.CompilerParams(dimension_semantics=("arbitrary",)),
-        cost_estimate=cost(rows * heads * (slash_count + 1), rows * width * 8),
+        input_output_aliases={9: 0} if done else {},
+        cost_estimate=cost(rows * len(heads) * (slash_count + 1), rows * width * 4),
         name="near",
-    )(slash, base, queries, queries, far, third, second, first, own)
-
-
-def vertical_kernel(count, slot_ref, ok_ref, quarters_ref, *refs):
-    ins, refs = refs[:8], refs[8:]
-    colours, refs = (refs[:5], refs[5:10]), refs[10:]
-    outs, (columns, score_a, score_b, top_a, top_b, stat_a, stat_b, sems) = refs[:2], refs[2:]
+    )(slash, base, queries, queries, fourth, third, second, first, own, *done)
+
+
+def choose(index, options, action):
+    if len(options) == 1:
+        action(options[0])
+        return
+    middle = len(options) // 2
+
+    @pl.when(index < middle)
+    def _():
+        choose(index, options[:middle], action)
+
+    @pl.when(index >= middle)
+    def _():
+        choose(index - middle, options[middle:], action)
+
+
+def vertical_kernel(count, quarter_count, piece_count, slot_ref, ok_ref, quarters_ref, *refs):
+    ins, refs = refs[: 4 * quarter_count], refs[4 * quarter_count :]
+    qs, next_qs, near_parts, stats = (ins[n::4] for n in range(4))
+    pieces, refs = refs[:piece_count], refs[piece_count:]
+    outs, (columns, score_a, score_b, top_a, top_b, stat_a, stat_b, sems) = refs[:quarter_count], refs[quarter_count:]
     step = pl.program_id(0)
     heads = 2 * pl.num_programs(0)
     depth = columns.shape[0]
-    piece = colours[0][0].shape[0]
+    piece = pieces[0].shape[0]
     part_rows = outs[0].shape[0]
     blocks = part_rows // BLK
-    lanes = lax.broadcasted_iota(jnp.int32, (2 * part_rows, HD), 1)
+    lanes = lax.broadcasted_iota(jnp.int32, (quarter_count * part_rows, HD), 1)
     buffers = ((score_a, top_a, stat_a), (score_b, top_b, stat_b))
 
     def fetch(which):
         place = which % depth
         for k in range(count):
             slot = slot_ref[which * count + k]
-            colour, region, inner = slot // (4 * piece), slot // piece % 4, slot % piece
-            half = piece // 2
-            for number, (own, ahead, low, high, behind) in enumerate(colours):
-
-                @pl.when(colour == number)
-                def _(own=own, ahead=ahead, low=low, high=high, behind=behind, k=k, region=region, inner=inner):
-                    def take(condition, source, index):
-                        @pl.when(condition)
-                        def _():
-                            pltpu.make_async_copy(source.at[index], columns.at[place, k], sems.at[place]).start()
-
-                    take(region == 0, own, inner)
-                    take(region == 1, ahead, inner)
-                    take((region == 2) & (inner < half), low, inner)
-                    take((region == 2) & (inner >= half), high, inner - half)
-                    take(region == 3, behind, inner)
+            inner = slot % piece
+
+            def take(source, k=k, inner=inner):
+                pltpu.make_async_copy(source.at[inner], columns.at[place, k], sems.at[place]).start()
+
+            choose(slot // piece, pieces, take)
 
     def arrive(which):
         place = which % depth
@@ -247,13 +257,13 @@
     def begin(which, qs, buffer):
         score_ref, top_ref, stat_ref = buffer
         biases = []
-        for part in range(2):
+        for part in range(quarter_count):
             for block in range(blocks):
                 here = quarters_ref[part] * blocks + block
                 flags = [ok_ref[which, here * count + k] > 0 for k in range(count)]
                 biases.append(bias_columns(flags, BLK))
         left = jnp.concatenate([jnp.concatenate(qs, axis=0), jnp.concatenate(biases, axis=0)], axis=1)
-        stat = jnp.concatenate([ins[3][...], ins[7][...]], axis=0)
+        stat = jnp.concatenate([stat[...] for stat in stats], axis=0)
         top = jnp.sum(jnp.where(lanes == which, stat, 0.0), axis=1, keepdims=True)
         stat_ref[...] = jnp.broadcast_to(top, stat_ref.shape)
         tops = []
@@ -271,37 +281,38 @@
         score_ref, top_ref, stat_ref = buffer
         mixed = weight_stage(score_ref, top_ref, [columns[which % depth, k, BLK:] for k in range(count)])
         weight = jnp.exp2(stat_ref[...] - top_ref[...])
-        near_part = jnp.concatenate([ins[2][:, local], ins[6][:, local]], axis=0)
+        near_part = jnp.concatenate([part[:, local] for part in near_parts], axis=0)
         whole = (mixed[:, :HD] + near_part * weight) / (mixed[:, HD:] + weight)
-        for part in range(2):
-            outs[part][:, local] = whole[part * part_rows : (part + 1) * part_rows].astype(outs[part].dtype)
+        for part, out_ref in enumerate(outs):
+            out_ref[:, local] = whole[part * part_rows : (part + 1) * part_rows].astype(out_ref.dtype)
 
     first, second = slice(0, HD), slice(HD, 2 * HD)
 
     @pl.when(step == 0)
     def _():
-        for which in range(3):
-            fetch(which)
+        fetch(0)
         arrive(0)
-        begin(0, [ins[0][:, first], ins[4][:, first]], buffers[0])
+        fetch(1)
+        fetch(2)
+        begin(0, [q[:, first] for q in qs], buffers[0])
 
     for offset in (1, 2):
         guarded(arrive, 2 * step + offset)
     for offset in (3, 4):
         guarded(fetch, 2 * step + offset)
-    begin(2 * step + 1, [ins[0][:, second], ins[4][:, second]], buffers[1])
+    begin(2 * step + 1, [q[:, second] for q in qs], buffers[1])
     finish(2 * step, first, buffers[0])
-    begin(jnp.minimum(2 * step + 2, heads - 1), [ins[1][...], ins[5][...]], buffers[0])
+    begin(jnp.minimum(2 * step + 2, heads - 1), [q[...] for q in next_qs], buffers[0])
     finish(2 * step + 1, second, buffers[1])
 
 
-def vertical_half(slots, ok, quarters, queries, near_part, stat, last_z, last_x):
+def vertical_quarters(slots, ok, quarters, queries, near_part, stat, pieces):
     rows, width = queries.shape
     heads = width // HD
     count = slots.shape[0] // heads
     part = rows // 4
+    quarter_count = quarters.shape[0]
     assert heads % 2 == 0 and heads > 2 and count % 2 == 0
-    hbm = pl.BlockSpec(memory_space=pl.ANY)
 
     def own(which, lanes, column):
         return pl.BlockSpec((part, lanes), lambda t, slot, ok, quarters: (quarters[which], column(t)))
@@ -315,22 +326,23 @@
         ]
 
     return pl.pallas_call(
-        functools.partial(vertical_kernel, count),
+        functools.partial(vertical_kernel, count, quarter_count, len(pieces)),
         grid_spec=pltpu.PrefetchScalarGridSpec(
             num_scalar_prefetch=3,
             grid=(heads // 2,),
-            in_specs=mine(0) + mine(1) + [hbm] * 10,
-            out_specs=[pl.BlockSpec((part, 2 * HD), lambda t, *_: (0, t))] * 2,
+            in_specs=[spec for which in range(quarter_count) for spec in mine(which)]
+            + [pl.BlockSpec(memory_space=pl.ANY)] * len(pieces),
+            out_specs=[pl.BlockSpec((part, 2 * HD), lambda t, *_: (0, t))] * quarter_count,
             scratch_shapes=[pltpu.VMEM((6, count, 2 * BLK, HD), jnp.bfloat16)]
-            + [pltpu.VMEM((2 * part, count * BLK), jnp.float32)] * 2
-            + [pltpu.VMEM((2 * part, HD), jnp.float32)] * 4
+            + [pltpu.VMEM((quarter_count * part, count * BLK), jnp.float32)] * 2
+            + [pltpu.VMEM((quarter_count * part, HD), jnp.float32)] * 4
             + [pltpu.SemaphoreType.DMA((6,))],
         ),
-        out_shape=[jax.ShapeDtypeStruct((part, width), jnp.bfloat16)] * 2,
+        out_shape=[jax.ShapeDtypeStruct((part, width), jnp.bfloat16)] * quarter_count,
         compiler_params=pltpu.CompilerParams(dimension_semantics=("arbitrary",)),
-        cost_estimate=cost(2 * part * heads * count, part * width * 32),
+        cost_estimate=cost(quarter_count * part * heads * count, quarter_count * part * width * 16),
         name="vertical",
-    )(slots, ok, quarters, *([queries, queries, near_part, stat] * 2), *last_z, *last_x)
+    )(slots, ok, quarters, *([queries, queries, near_part, stat] * quarter_count), *pieces)
 
 
 def tables(vertical, slash, slab_index, slab_blocks):
@@ -361,14 +373,15 @@
 
 
 def along(array, axis):
-    return jnp.concatenate([array] + [from_ahead(array, axis, by) for by in (1, 2, 3)], axis=0)
-
-
-def around(array, axis):
-    half = array.shape[0] // 2
-    ahead, behind = from_ahead(array, axis, 1), from_ahead(array, axis, 3)
-    low, high = from_ahead(ahead[:half], axis, 1), from_ahead(behind[half:], axis, 3)
-    return [array, ahead, low, high, behind]
+    one, two, three = (from_ahead(array, axis, by) for by in (1, 2, 3))
+    return jnp.concatenate([array, one], axis=0), jnp.concatenate([two, three], axis=0)
+
+
+def around(halves, axis):
+    ahead, behind = from_ahead(halves[0], axis, 1), from_ahead(halves[1], axis, 3)
+    ahead_rest, behind_rest = from_ahead(halves[1], axis, 1), from_ahead(halves[0], axis, 3)
+    low, high = from_ahead(ahead, axis, 1), from_ahead(behind, axis, 3)
+    return [*halves, ahead, ahead_rest, low, high, behind_rest, behind]
 
 
 def step(queries, keys, values, vertical, slash):
@@ -388,31 +401,34 @@
 
     half = CAP // 2
     other = swapped(packed)
-    last_z = around(along(jnp.concatenate([packed[:half], other[:half]], axis=0), "x"), "z")
-    last_x = around(along(jnp.concatenate([packed[half:], other[half:]], axis=0), "z"), "x")
+    over_x = along(jnp.concatenate([packed[:half], other[:half]], axis=0), "x")
+    over_z = along(jnp.concatenate([packed[half:], other[half:]], axis=0), "z")
+    pieces = around(over_x, "z") + around(over_z, "x")
     upper = lax.axis_index("y") == 1
     second, fourth = from_before(kv, 1), from_before(kv, 2)
     first = swapped(jnp.where(upper, second, kv))
     third = swapped(jnp.where(upper, *lax.optimization_barrier((fourth, second))))
-    far = fourth[slab_blocks - REACH % slab_blocks :]
     slots, ok = tables(vertical, slash, slab_index, slab_blocks)
-    near_part, stat = near(slash, base, queries, far, third, second, first, kv)
+    heads = vertical.shape[0]
+    near_args = (slash, base, queries, fourth, third, second, first, kv)
+    state = near(*near_args, range(heads // 2))
+    near_part, stat = near(*near_args, range(heads // 2, heads), state)
     here = lax.axis_index("head").astype(jnp.int32)
 
-    def half(pair):
-        quarters = jnp.stack([here ^ step for step in pair])
-        return vertical_half(slots, ok, quarters, queries, near_part, stat, last_z, last_x)
+    def done(*steps):
+        quarters = jnp.stack([here ^ step for step in steps])
+        return vertical_quarters(slots, ok, quarters, queries, near_part, stat, pieces)
 
     def sent(piece, step):
         return lax.ppermute(piece, "head", [(i, i ^ step) for i in range(parts)])
 
-    second_piece, third_piece = half((2, 3))
-    first_piece, own_piece = half((1, 0))
-    pieces = [own_piece, sent(first_piece, 1), sent(second_piece, 2), sent(third_piece, 3)]
+    second_piece, third_piece = done(2, 3)
+    first_piece, own_piece = done(1, 0)
+    outs = [own_piece, sent(first_piece, 1), sent(second_piece, 2), sent(third_piece, 3)]
     width = queries.shape[1]
-    out = jnp.zeros((pieces[0].shape[0], width * parts), pieces[0].dtype)
+    out = jnp.zeros((own_piece.shape[0], width * parts), own_piece.dtype)
     for step in (0, 1, 2, 3):
-        out = lax.dynamic_update_slice_in_dim(out, pieces[step], (here ^ step) * width, 1)
+        out = lax.dynamic_update_slice_in_dim(out, outs[step], (here ^ step) * width, 1)
     return out
 
 

time: 162 us -> 176 us (1.086)
  the two profiles are of different devices: /device:TPU:2 before, /device:TPU:1 now
where the time goes in v2:
time: 176 us; the launch traced here: 175 us
  starting transfers between devices  54.8 us (31%)
  waiting for transfers between devices  54.5 us (31%)
  Pallas kernels  52 us (30%)
  other arithmetic  9.79 us (6%)
  local copies, waits for them, and re-layouts  3.46 us (2%)
    ppermute x18, starting transfers between devices, from_ahead(): lax.ppermute(array, axis, [((i + by) % size, i) for i in range(size)])  38.3 us
    pallas_call x2, Pallas kernels, vertical_quarters(): pl.pallas_call(functools.partial(vertical_kernel, count, quarter_count, l...  24.6 us
    pallas_call x2, Pallas kernels, near(): pl.pallas_call(functools.partial(near_kernel, first_head), grid_spec=pltp...  24.1 us
    ppermute x3, waiting for transfers between devices, sent(): return lax.ppermute(piece, 'head', [(i, i ^ step) for i in range(parts)])  23 us
    ppermute x18, waiting for transfers between devices, from_ahead(): lax.ppermute(array, axis, [((i + by) % size, i) for i in range(size)])  15.9 us
    ppermute x2, waiting for transfers between devices, from_before(): lax.ppermute(array, SEQ, [(i, (i + pairs * pair) % slabs) for i in range(...  13.1 us
    ppermute x3, starting transfers between devices, sent(): return lax.ppermute(piece, 'head', [(i, i ^ step) for i in range(parts)])  7.86 us
    ppermute x2, starting transfers between devices, from_before(): lax.ppermute(array, SEQ, [(i, (i + pairs * pair) % slabs) for i in range(...  5.76 us
  transfers between devices with their start and end apart: 26, of which 8 were waited for; matrix products, arithmetic and copies ran while one was open for 7% of the time, Pallas kernels for 21%

profile of v2, /device:TPU:1, one launch (start us, length us, event | category | flops | bytes accessed | tf_op | source)
XLA Modules:
  0.0 175.0 jit_solution(13273531146556352767)
XLA Ops:
  0.0 3.3 %prep.1 = (bf16[8,256,128]{2,1,0:T(8,128)(2,1)}, bf16[4,256,128]{2,1,0:T(8,128)(2,1)}) custom-call(s32[8,8]{1,0:T(8,128)} %vertical_ref.1, s32[1]{0:T(128)} %bitcast.2.base_ref, bf16[1024,128]{1,0:T(8,128)(2,1)} %keys_ref.1, bf16[1024,128]{1,0:T(8,128)(2,1)} %values_ref.1), custom_call_target="tpu_custom_call" | custom-call | tf_op jit(solution)/shard_map/prep/pallas_call | solution.py:53
  3.3 2.5 %collective-permute-start.1 = (bf16[8,256,128]{2,1,0:T(8,128)(2,1)}, bf16[8,256,128]{2,1,0:T(8,128)(2,1)S(1)}, u32[]{:S(2)}, u32[]{:S(2)}) collective-permute-start(bf16[8,256,128]{2,1,0:T(8,128)(2,1)} %get-tuple-element.17.own_ref), channel_id=1, source_target_pairs={{0,2},{1,3},{2,4},{3,5},{4,6},{5,7},{6,8},{7,9},{8,10},{9,11},{10,... | collective-permute-start | bytes 1572872 | tf_op jit(solution)/shard_map/ppermute | solution.py:400
  5.7 3.3 %collective-permute-start = (bf16[8,256,128]{2,1,0:T(8,128)(2,1)}, bf16[8,256,128]{2,1,0:T(8,128)(2,1)S(1)}, u32[]{:S(2)}, u32[]{:S(2)}) collective-permute-start(bf16[8,256,128]{2,1,0:T(8,128)(2,1)} %get-tuple-element.17.own_ref), channel_id=1, source_target_pairs={{0,4},{1,5},{2,6},{3,7},{4,8},{5,9},{6,10},{7,11},{8,12},{9,13},{1... | collective-permute-start | bytes 1572872 | tf_op jit(solution)/shard_map/ppermute | solution.py:400
  9.0 1.3 collective-permute-start.4
  10.3 1.0 fusion.12
  13.5 2.4 %collective-permute-done.4 = bf16[4,256,128]{2,1,0:T(8,128)(2,1)S(1)} collective-permute-done((bf16[4,256,128]{2,1,0:T(8,128)(2,1)}, bf16[4,256,128]{2,1,0:T(8,128)(2,1)S(1)}, u32[]{:S(2)}, u32[]{:S(2)}) %collective-permute-start.4) | collective-permute-done | bytes 262176 | tf_op jit(solution)/shard_map/ppermute | solution.py:397
  15.9 2.8 %collective-permute-start.6 = (bf16[4,256,128]{2,1,0:T(8,128)(2,1)S(1)}, bf16[4,256,128]{2,1,0:T(8,128)(2,1)S(1)}, u32[]{:S(2)}, u32[]{:S(2)}) collective-permute-start(bf16[4,256,128]{2,1,0:T(8,128)(2,1)S(1)} %pad_maximum_fusion.2), channel_id=1, source_target_pairs={{16,0},{24,8},{0,16},{8,24},{17,1},{25,9},{1,17},{9,25},{18,2},{26... | collective-permute-start | bytes 786440 | tf_op jit(solution)/shard_map/ppermute | solution.py:372
  19.5 11.0 %collective-permute-done.1.second_ref = bf16[8,256,128]{2,1,0:T(8,128)(2,1)S(1)} collective-permute-done((bf16[8,256,128]{2,1,0:T(8,128)(2,1)}, bf16[8,256,128]{2,1,0:T(8,128)(2,1)S(1)}, u32[]{:S(2)}, u32[]{:S(2)}) %collective-permute-start.1) | collective-permute-done | bytes 524320 | tf_op jit(solution)/shard_map/ppermute | solution.py:400
  30.5 2.1 %collective-permute-done.far_ref = bf16[8,256,128]{2,1,0:T(8,128)(2,1)S(1)} collective-permute-done((bf16[8,256,128]{2,1,0:T(8,128)(2,1)}, bf16[8,256,128]{2,1,0:T(8,128)(2,1)S(1)}, u32[]{:S(2)}, u32[]{:S(2)}) %collective-permute-start) | collective-permute-done | bytes 524320 | tf_op jit(solution)/shard_map/ppermute | solution.py:400
  34.8 1.3 collective-permute-start.2
  36.4 3.2 %collective-permute-done.15 = bf16[4,256,128]{2,1,0:T(8,128)(2,1)S(1)} collective-permute-done((bf16[4,256,128]{2,1,0:T(8,128)(2,1)S(1)}, bf16[4,256,128]{2,1,0:T(8,128)(2,1)S(1)}, u32[]{:S(2)}, u32[]{:S(2)}) %collective-permute-start.15) | collective-permute-done | bytes 262176 | tf_op jit(solution)/shard_map/ppermute | solution.py:372
  39.6 7.9 %collective-permute-start.11 = (bf16[8,256,128]{2,1,0:T(8,128)(2,1)S(1)}, bf16[8,256,128]{2,1,0:T(8,128)(2,1)S(1)}, u32[]{:S(2)}, u32[]{:S(2)}) collective-permute-start(bf16[8,256,128]{2,1,0:T(8,128)(2,1)S(1)} %constant_dynamic-update-slice_fusion.refs_9_), channel_id=1, source_target_pairs={{6,0},{0,2},{2,4},{4,6},{7,1},{1,3},{3,5},{5,7},{14,8},{8,10},{10,... | collective-permute-start | bytes 1572872 | tf_op jit(solution)/shard_map/ppermute | solution.py:372
  47.7 1.3 compare_reduce_fusion
  48.9 7.2 %collective-permute-start.14 = (bf16[4,256,128]{2,1,0:T(8,128)(2,1)S(1)}, bf16[4,256,128]{2,1,0:T(8,128)(2,1)}, u32[]{:S(2)}, u32[]{:S(2)}) collective-permute-start(bf16[4,256,128]{2,1,0:T(8,128)(2,1)S(1)} %pad_maximum_fusion.3), channel_id=1, source_target_pairs={{2,0},{4,2},{6,4},{0,6},{3,1},{5,3},{7,5},{1,7},{10,8},{12,10},{14... | collective-permute-start | bytes 786440 | tf_op jit(solution)/shard_map/ppermute | solution.py:372
  57.2 1.0 pad_maximum_fusion.refs_8_
  58.2 1.9 %collective-permute-done.14 = bf16[4,256,128]{2,1,0:T(8,128)(2,1)} collective-permute-done((bf16[4,256,128]{2,1,0:T(8,128)(2,1)S(1)}, bf16[4,256,128]{2,1,0:T(8,128)(2,1)}, u32[]{:S(2)}, u32[]{:S(2)}) %collective-permute-start.14) | collective-permute-done | bytes 262176 | tf_op jit(solution)/shard_map/ppermute | solution.py:372
  60.1 2.2 %collective-permute-start.18 = (bf16[8,256,128]{2,1,0:T(8,128)(2,1)S(1)}, bf16[8,256,128]{2,1,0:T(8,128)(2,1)S(1)}, u32[]{:S(2)}, u32[]{:S(2)}) collective-permute-start(bf16[8,256,128]{2,1,0:T(8,128)(2,1)S(1)} %constant_dynamic-update-slice_fusion.2.refs_17_), channel_id=1, source_target_pairs={{8,0},{16,8},{24,16},{0,24},{9,1},{17,9},{25,17},{1,25},{10,2},{18... | collective-permute-start | bytes 1572872 | tf_op jit(solution)/shard_map/ppermute | solution.py:372
  62.3 1.0 pad_maximum_fusion.1.refs_16_
  63.3 3.6 %collective-permute-start.9 = (bf16[8,256,128]{2,1,0:T(8,128)(2,1)S(1)}, bf16[8,256,128]{2,1,0:T(8,128)(2,1)S(1)}, u32[]{:S(2)}, u32[]{:S(2)}) collective-permute-start(bf16[8,256,128]{2,1,0:T(8,128)(2,1)S(1)} %constant_dynamic-update-slice_fusion.refs_9_), channel_id=1, source_target_pairs={{2,0},{4,2},{6,4},{0,6},{3,1},{5,3},{7,5},{1,7},{10,8},{12,10},{14... | collective-permute-start | bytes 1572872 | tf_op jit(solution)/shard_map/ppermute | solution.py:372
  66.9 5.1 %collective-permute-start.8 = (bf16[8,256,128]{2,1,0:T(8,128)(2,1)S(1)}, bf16[8,256,128]{2,1,0:T(8,128)(2,1)}, u32[]{:S(2)}, u32[]{:S(2)}) collective-permute-start(bf16[8,256,128]{2,1,0:T(8,128)(2,1)S(1)} %pad_maximum_fusion.refs_8_), channel_id=1, source_target_pairs={{2,0},{4,2},{6,4},{0,6},{3,1},{5,3},{7,5},{1,7},{10,8},{12,10},{14... | collective-permute-start | bytes 1572872 | tf_op jit(solution)/shard_map/ppermute | solution.py:372
  74.2 1.4 collective-permute-start.22
  76.0 10.9 %collective-permute-done.8.refs_10_ = bf16[8,256,128]{2,1,0:T(8,128)(2,1)} collective-permute-done((bf16[8,256,128]{2,1,0:T(8,128)(2,1)S(1)}, bf16[8,256,128]{2,1,0:T(8,128)(2,1)}, u32[]{:S(2)}, u32[]{:S(2)}) %collective-permute-start.8) | collective-permute-done | bytes 524320 | tf_op jit(solution)/shard_map/ppermute | solution.py:372
  86.8 3.5 %collective-permute-start.10 = (bf16[8,256,128]{2,1,0:T(8,128)(2,1)}, bf16[8,256,128]{2,1,0:T(8,128)(2,1)}, u32[]{:S(2)}, u32[]{:S(2)}) collective-permute-start(bf16[8,256,128]{2,1,0:T(8,128)(2,1)} %collective-permute-done.8.refs_10_), channel_id=1, source_target_pairs={{2,0},{4,2},{6,4},{0,6},{3,1},{5,3},{7,5},{1,7},{10,8},{12,10},{14... | collective-permute-start | bytes 1572872 | tf_op jit(solution)/shard_map/ppermute | solution.py:372
  90.4 2.9 %collective-permute-start.19 = (bf16[8,256,128]{2,1,0:T(8,128)(2,1)}, bf16[8,256,128]{2,1,0:T(8,128)(2,1)}, u32[]{:S(2)}, u32[]{:S(2)}) collective-permute-start(bf16[8,256,128]{2,1,0:T(8,128)(2,1)} %collective-permute-done.17.refs_18_), channel_id=1, source_target_pairs={{8,0},{16,8},{24,16},{0,24},{9,1},{17,9},{25,17},{1,25},{10,2},{18... | collective-permute-start | bytes 1572872 | tf_op jit(solution)/shard_map/ppermute | solution.py:372
  93.9 11.9 %near.2 = (f32[1024,1024]{1,0:T(8,128)}, f32[1024,128]{1,0:T(8,128)}) custom-call(s32[8,8]{1,0:T(8,128)} %slash_ref.3, s32[1]{0:T(128)} %bitcast.2.base_ref, bf16[1024,1024]{1,0:T(8,128)(2,1)} %refs_5_.3, bf16[1024,1024]{1,0:T(8,128)(2,1)} %refs_5_.3, bf16[8,256,128]{2,1,0:T(8,128)(2,1)} %copy-done.12, ...), custom_call_target="tpu_custom_call" | custom-call | flops 2415919104 | bytes 4194304 | tf_op jit(solution)/shard_map/near/pallas_call | solution.py:173
  105.9 12.2 %near.3 = (f32[1024,1024]{1,0:T(8,128)}, f32[1024,128]{1,0:T(8,128)}) custom-call(s32[8,8]{1,0:T(8,128)} %slash_ref.3, s32[1]{0:T(128)} %bitcast.2.base_ref, bf16[1024,1024]{1,0:T(8,128)(2,1)} %refs_5_.3, bf16[1024,1024]{1,0:T(8,128)(2,1)} %refs_5_.3, bf16[8,256,128]{2,1,0:T(8,128)(2,1)} %copy-done.12, ...), custom_call_target="tpu_custom_call", output_to_operand_aliasing={{0}: (9, {})} | custom-call | flops 2415919104 | bytes 4194304 | tf_op jit(solution)/shard_map/near/pallas_call | solution.py:173
  118.2 12.3 %vertical.2 = (bf16[256,1024]{1,0:T(8,128)(2,1)}, bf16[256,1024]{1,0:T(8,128)(2,1)}) custom-call(s32[64]{0:T(128)} %fusion.5.slot_ref, s32[8,64]{1,0:T(8,128)} %fusion.4.ok_ref, s32[2]{0:T(128)} %get-tuple-element.33.quarters_ref, bf16[1024,1024]{1,0:T(8,128)(2,1)} %refs_5_.3, bf16[1024,1024]{1,0:T(8,128)(2,1)} %refs_5_.3, ...), custom_call_target="tpu_custom_call" | custom-call | flops 2147483648 | bytes 8388608 | tf_op jit(solution)/shard_map/vertical/pallas_call | solution.py:328
  130.5 4.6 %collective-permute-start.23 = (bf16[256,1024]{1,0:T(8,128)(2,1)}, bf16[256,1024]{1,0:T(8,128)(2,1)S(1)}, u32[]{:S(2)}, u32[]{:S(2)}) collective-permute-start(bf16[256,1024]{1,0:T(8,128)(2,1)} %get-tuple-element.26), channel_id=1, source_target_pairs={{0,32},{32,0},{64,96},{96,64},{1,33},{33,1},{65,97},{97,65},{2,34}... | collective-permute-start | bytes 1572872 | tf_op jit(solution)/shard_map/ppermute | solution.py:423
  135.1 12.3 %vertical.3 = (bf16[256,1024]{1,0:T(8,128)(2,1)}, bf16[256,1024]{1,0:T(8,128)(2,1)}) custom-call(s32[64]{0:T(128)} %fusion.5.slot_ref, s32[8,64]{1,0:T(8,128)} %fusion.4.ok_ref, s32[2]{0:T(128)} %get-tuple-element.34.quarters_ref, bf16[1024,1024]{1,0:T(8,128)(2,1)} %refs_5_.3, bf16[1024,1024]{1,0:T(8,128)(2,1)} %refs_5_.3, ...), custom_call_target="tpu_custom_call" | custom-call | flops 2147483648 | bytes 8388608 | tf_op jit(solution)/shard_map/vertical/pallas_call | solution.py:328
  147.5 2.9 %collective-permute-start.24 = (bf16[256,1024]{1,0:T(8,128)(2,1)}, bf16[256,1024]{1,0:T(8,128)(2,1)S(1)}, u32[]{:S(2)}, u32[]{:S(2)}) collective-permute-start(bf16[256,1024]{1,0:T(8,128)(2,1)} %get-tuple-element.27), channel_id=1, source_target_pairs={{0,64},{32,96},{64,0},{96,32},{1,65},{33,97},{65,1},{97,33},{2,66}... | collective-permute-start | bytes 1572872 | tf_op jit(solution)/shard_map/ppermute | solution.py:423
  151.1 11.6 %collective-permute-done.24 = bf16[256,1024]{1,0:T(8,128)(2,1)S(1)} collective-permute-done((bf16[256,1024]{1,0:T(8,128)(2,1)}, bf16[256,1024]{1,0:T(8,128)(2,1)S(1)}, u32[]{:S(2)}, u32[]{:S(2)}) %collective-permute-start.24) | collective-permute-done | bytes 524320 | tf_op jit(solution)/shard_map/ppermute | solution.py:423
  162.8 11.4 %collective-permute-done.25 = bf16[256,1024]{1,0:T(8,128)(2,1)S(1)} collective-permute-done((bf16[256,1024]{1,0:T(8,128)(2,1)}, bf16[256,1024]{1,0:T(8,128)(2,1)S(1)}, u32[]{:S(2)}, u32[]{:S(2)}) %collective-permute-start.25) | collective-permute-done | bytes 524320 | tf_op jit(solution)/shard_map/ppermute | solution.py:423
  (93 shorter events, 11.4 us)
Async XLA Ops:
  3.3 27.2 %collective-permute-start.1 = (bf16[8,256,128]{2,1,0:T(8,128)(2,1)}, bf16[8,256,128]{2,1,0:T(8,128)(2,1)S(1)}, u32[]{:S(2)}, u32[]{:S(2)}) collective-permute-start(bf16[8,256,128]{2,1,0:T(8,128)(2,1)} %get-tuple-element.17.own_ref), channel_id=1, source_target_pairs={{0,2},{1,3},{2,4},{3,5},{4,6},{5,7},{6,8},{7,9},{8,10},{9,11},{10,... | collective-permute-start | bytes 1572872 | tf_op jit(solution)/shard_map/ppermute | solution.py:400
  5.7 26.9 %collective-permute-start = (bf16[8,256,128]{2,1,0:T(8,128)(2,1)}, bf16[8,256,128]{2,1,0:T(8,128)(2,1)S(1)}, u32[]{:S(2)}, u32[]{:S(2)}) collective-permute-start(bf16[8,256,128]{2,1,0:T(8,128)(2,1)} %get-tuple-element.17.own_ref), channel_id=1, source_target_pairs={{0,4},{1,5},{2,6},{3,7},{4,8},{5,9},{6,10},{7,11},{8,12},{9,13},{1... | collective-permute-start | bytes 1572872 | tf_op jit(solution)/shard_map/ppermute | solution.py:400
  9.0 6.9 %collective-permute-start.4 = (bf16[4,256,128]{2,1,0:T(8,128)(2,1)}, bf16[4,256,128]{2,1,0:T(8,128)(2,1)S(1)}, u32[]{:S(2)}, u32[]{:S(2)}) collective-permute-start(bf16[4,256,128]{2,1,0:T(8,128)(2,1)} %get-tuple-element.24), channel_id=1, source_target_pairs={{0,1},{1,0},{2,3},{3,2},{4,5},{5,4},{6,7},{7,6},{8,9},{9,8},{10,11... | collective-permute-start | bytes 786440 | tf_op jit(solution)/shard_map/ppermute | solution.py:397
  15.9 18.8 %collective-permute-start.6 = (bf16[4,256,128]{2,1,0:T(8,128)(2,1)S(1)}, bf16[4,256,128]{2,1,0:T(8,128)(2,1)S(1)}, u32[]{:S(2)}, u32[]{:S(2)}) collective-permute-start(bf16[4,256,128]{2,1,0:T(8,128)(2,1)S(1)} %pad_maximum_fusion.2), channel_id=1, source_target_pairs={{16,0},{24,8},{0,16},{8,24},{17,1},{25,9},{1,17},{9,25},{18,2},{26... | collective-permute-start | bytes 786440 | tf_op jit(solution)/shard_map/ppermute | solution.py:372
  18.7 17.3 %collective-permute-start.7 = (bf16[4,256,128]{2,1,0:T(8,128)(2,1)S(1)}, bf16[4,256,128]{2,1,0:T(8,128)(2,1)S(1)}, u32[]{:S(2)}, u32[]{:S(2)}) collective-permute-start(bf16[4,256,128]{2,1,0:T(8,128)(2,1)S(1)} %pad_maximum_fusion.2), channel_id=1, source_target_pairs={{24,0},{0,8},{8,16},{16,24},{25,1},{1,9},{9,17},{17,25},{26,2},{2,... | collective-permute-start | bytes 786440 | tf_op jit(solution)/shard_map/ppermute | solution.py:372
  19.1 20.5 %collective-permute-start.15 = (bf16[4,256,128]{2,1,0:T(8,128)(2,1)S(1)}, bf16[4,256,128]{2,1,0:T(8,128)(2,1)S(1)}, u32[]{:S(2)}, u32[]{:S(2)}) collective-permute-start(bf16[4,256,128]{2,1,0:T(8,128)(2,1)S(1)} %pad_maximum_fusion.3), channel_id=1, source_target_pairs={{4,0},{6,2},{0,4},{2,6},{5,1},{7,3},{1,5},{3,7},{12,8},{14,10},{8,... | collective-permute-start | bytes 786440 | tf_op jit(solution)/shard_map/ppermute | solution.py:372
  30.5 17.1 %collective-permute-start.16 = (bf16[4,256,128]{2,1,0:T(8,128)(2,1)S(1)}, bf16[4,256,128]{2,1,0:T(8,128)(2,1)S(1)}, u32[]{:S(2)}, u32[]{:S(2)}) collective-permute-start(bf16[4,256,128]{2,1,0:T(8,128)(2,1)S(1)} %pad_maximum_fusion.3), channel_id=1, source_target_pairs={{6,0},{0,2},{2,4},{4,6},{7,1},{1,3},{3,5},{5,7},{14,8},{8,10},{10,... | collective-permute-start | bytes 786440 | tf_op jit(solution)/shard_map/ppermute | solution.py:372
  32.6 16.3 %collective-permute-start.5 = (bf16[4,256,128]{2,1,0:T(8,128)(2,1)S(1)}, bf16[4,256,128]{2,1,0:T(8,128)(2,1)}, u32[]{:S(2)}, u32[]{:S(2)}) collective-permute-start(bf16[4,256,128]{2,1,0:T(8,128)(2,1)S(1)} %pad_maximum_fusion.2), channel_id=1, source_target_pairs={{8,0},{16,8},{24,16},{0,24},{9,1},{17,9},{25,17},{1,25},{10,2},{18... | collective-permute-start | bytes 786440 | tf_op jit(solution)/shard_map/ppermute | solution.py:372
  34.8 28.5 %collective-permute-start.2 = (bf16[8,256,128]{2,1,0:T(8,128)(2,1)}, bf16[8,256,128]{2,1,0:T(8,128)(2,1)}, u32[]{:S(2)}, u32[]{:S(2)}) collective-permute-start(bf16[8,256,128]{2,1,0:T(8,128)(2,1)} %broadcast_select_fusion.1), channel_id=1, source_target_pairs={{0,1},{1,0},{2,3},{3,2},{4,5},{5,4},{6,7},{7,6},{8,9},{9,8},{10,11... | collective-permute-start | bytes 1572872 | tf_op jit(solution)/shard_map/ppermute | solution.py:397
  36.1 30.8 %collective-permute-start.3 = (bf16[8,256,128]{2,1,0:T(8,128)(2,1)}, bf16[8,256,128]{2,1,0:T(8,128)(2,1)}, u32[]{:S(2)}, u32[]{:S(2)}) collective-permute-start(bf16[8,256,128]{2,1,0:T(8,128)(2,1)} %broadcast_select_fusion), channel_id=1, source_target_pairs={{0,1},{1,0},{2,3},{3,2},{4,5},{5,4},{6,7},{7,6},{8,9},{9,8},{10,11... | collective-permute-start | bytes 1572872 | tf_op jit(solution)/shard_map/ppermute | solution.py:397
  36.4 69.5 %copy-start.3 = (bf16[8,256,128]{2,1,0:T(8,128)(2,1)}, bf16[8,256,128]{2,1,0:T(8,128)(2,1)S(1)}, u32[]{:S(2)}) copy-start(bf16[8,256,128]{2,1,0:T(8,128)(2,1)S(1)} %constant_dynamic-update-slice_fusion.refs_9_) | copy-start | bytes 1572868
  39.6 32.4 %collective-permute-start.11 = (bf16[8,256,128]{2,1,0:T(8,128)(2,1)S(1)}, bf16[8,256,128]{2,1,0:T(8,128)(2,1)S(1)}, u32[]{:S(2)}, u32[]{:S(2)}) collective-permute-start(bf16[8,256,128]{2,1,0:T(8,128)(2,1)S(1)} %constant_dynamic-update-slice_fusion.refs_9_), channel_id=1, source_target_pairs={{6,0},{0,2},{2,4},{4,6},{7,1},{1,3},{3,5},{5,7},{14,8},{8,10},{10,... | collective-permute-start | bytes 1572872 | tf_op jit(solution)/shard_map/ppermute | solution.py:372
  47.6 58.3 %copy-start.4 = (bf16[8,256,128]{2,1,0:T(8,128)(2,1)}, bf16[8,256,128]{2,1,0:T(8,128)(2,1)S(1)}, u32[]{:S(2)}) copy-start(bf16[8,256,128]{2,1,0:T(8,128)(2,1)S(1)} %constant_dynamic-update-slice_fusion.2.refs_17_) | copy-start | bytes 1572868
  47.6 24.4 %collective-permute-start.20 = (bf16[8,256,128]{2,1,0:T(8,128)(2,1)S(1)}, bf16[8,256,128]{2,1,0:T(8,128)(2,1)S(1)}, u32[]{:S(2)}, u32[]{:S(2)}) collective-permute-start(bf16[8,256,128]{2,1,0:T(8,128)(2,1)S(1)} %constant_dynamic-update-slice_fusion.2.refs_17_), channel_id=1, source_target_pairs={{24,0},{0,8},{8,16},{16,24},{25,1},{1,9},{9,17},{17,25},{26,2},{2,... | collective-permute-start | bytes 1572872 | tf_op jit(solution)/shard_map/ppermute | solution.py:372
  48.9 11.1 %collective-permute-start.14 = (bf16[4,256,128]{2,1,0:T(8,128)(2,1)S(1)}, bf16[4,256,128]{2,1,0:T(8,128)(2,1)}, u32[]{:S(2)}, u32[]{:S(2)}) collective-permute-start(bf16[4,256,128]{2,1,0:T(8,128)(2,1)S(1)} %pad_maximum_fusion.3), channel_id=1, source_target_pairs={{2,0},{4,2},{6,4},{0,6},{3,1},{5,3},{7,5},{1,7},{10,8},{12,10},{14... | collective-permute-start | bytes 786440 | tf_op jit(solution)/shard_map/ppermute | solution.py:372
  58.2 47.7 %copy-start = (bf16[8,256,128]{2,1,0:T(8,128)(2,1)}, bf16[8,256,128]{2,1,0:T(8,128)(2,1)S(1)}, u32[]{:S(2)}) copy-start(bf16[8,256,128]{2,1,0:T(8,128)(2,1)S(1)} %pad_maximum_fusion.refs_8_) | copy-start | bytes 1572868
  60.1 14.1 %collective-permute-start.18 = (bf16[8,256,128]{2,1,0:T(8,128)(2,1)S(1)}, bf16[8,256,128]{2,1,0:T(8,128)(2,1)S(1)}, u32[]{:S(2)}, u32[]{:S(2)}) collective-permute-start(bf16[8,256,128]{2,1,0:T(8,128)(2,1)S(1)} %constant_dynamic-update-slice_fusion.2.refs_17_), channel_id=1, source_target_pairs={{8,0},{16,8},{24,16},{0,24},{9,1},{17,9},{25,17},{1,25},{10,2},{18... | collective-permute-start | bytes 1572872 | tf_op jit(solution)/shard_map/ppermute | solution.py:372
  63.3 42.6 %copy-start.1 = (bf16[8,256,128]{2,1,0:T(8,128)(2,1)}, bf16[8,256,128]{2,1,0:T(8,128)(2,1)S(1)}, u32[]{:S(2)}) copy-start(bf16[8,256,128]{2,1,0:T(8,128)(2,1)S(1)} %pad_maximum_fusion.1.refs_16_) | copy-start | bytes 1572868
  63.3 12.3 %collective-permute-start.9 = (bf16[8,256,128]{2,1,0:T(8,128)(2,1)S(1)}, bf16[8,256,128]{2,1,0:T(8,128)(2,1)S(1)}, u32[]{:S(2)}, u32[]{:S(2)}) collective-permute-start(bf16[8,256,128]{2,1,0:T(8,128)(2,1)S(1)} %constant_dynamic-update-slice_fusion.refs_9_), channel_id=1, source_target_pairs={{2,0},{4,2},{6,4},{0,6},{3,1},{5,3},{7,5},{1,7},{10,8},{12,10},{14... | collective-permute-start | bytes 1572872 | tf_op jit(solution)/shard_map/ppermute | solution.py:372
  66.9 19.9 %collective-permute-start.8 = (bf16[8,256,128]{2,1,0:T(8,128)(2,1)S(1)}, bf16[8,256,128]{2,1,0:T(8,128)(2,1)}, u32[]{:S(2)}, u32[]{:S(2)}) collective-permute-start(bf16[8,256,128]{2,1,0:T(8,128)(2,1)S(1)} %pad_maximum_fusion.refs_8_), channel_id=1, source_target_pairs={{2,0},{4,2},{6,4},{0,6},{3,1},{5,3},{7,5},{1,7},{10,8},{12,10},{14... | collective-permute-start | bytes 1572872 | tf_op jit(solution)/shard_map/ppermute | solution.py:372
  72.0 33.9 %copy-start.5 = (bf16[8,256,128]{2,1,0:T(8,128)(2,1)}, bf16[8,256,128]{2,1,0:T(8,128)(2,1)S(1)}, u32[]{:S(2)}) copy-start(bf16[8,256,128]{2,1,0:T(8,128)(2,1)S(1)} %collective-permute-done.11.refs_15_) | copy-start | bytes 1572868
  72.0 18.3 %collective-permute-start.13 = (bf16[8,256,128]{2,1,0:T(8,128)(2,1)S(1)}, bf16[8,256,128]{2,1,0:T(8,128)(2,1)S(1)}, u32[]{:S(2)}, u32[]{:S(2)}) collective-permute-start(bf16[8,256,128]{2,1,0:T(8,128)(2,1)S(1)} %pad_maximum_fusion.refs_8_), channel_id=1, source_target_pairs={{6,0},{0,2},{2,4},{4,6},{7,1},{1,3},{3,5},{5,7},{14,8},{8,10},{10,... | collective-permute-start | bytes 1572872 | tf_op jit(solution)/shard_map/ppermute | solution.py:372
  72.0 33.9 %copy-start.6 = (bf16[8,256,128]{2,1,0:T(8,128)(2,1)}, bf16[8,256,128]{2,1,0:T(8,128)(2,1)S(1)}, u32[]{:S(2)}) copy-start(bf16[8,256,128]{2,1,0:T(8,128)(2,1)S(1)} %collective-permute-done.20.refs_23_) | copy-start | bytes 1572868
  72.0 14.8 %collective-permute-start.17 = (bf16[8,256,128]{2,1,0:T(8,128)(2,1)S(1)}, bf16[8,256,128]{2,1,0:T(8,128)(2,1)}, u32[]{:S(2)}, u32[]{:S(2)}) collective-permute-start(bf16[8,256,128]{2,1,0:T(8,128)(2,1)S(1)} %pad_maximum_fusion.1.refs_16_), channel_id=1, source_target_pairs={{8,0},{16,8},{24,16},{0,24},{9,1},{17,9},{25,17},{1,25},{10,2},{18... | collective-permute-start | bytes 1572872 | tf_op jit(solution)/shard_map/ppermute | solution.py:372
  74.2 44.0 %collective-permute-start.22 = (bf16[8,256,128]{2,1,0:T(8,128)(2,1)S(1)}, bf16[8,256,128]{2,1,0:T(8,128)(2,1)}, u32[]{:S(2)}, u32[]{:S(2)}) collective-permute-start(bf16[8,256,128]{2,1,0:T(8,128)(2,1)S(1)} %pad_maximum_fusion.1.refs_16_), channel_id=1, source_target_pairs={{24,0},{0,8},{8,16},{16,24},{25,1},{1,9},{9,17},{17,25},{26,2},{2,... | collective-permute-start | bytes 1572872 | tf_op jit(solution)/shard_map/ppermute | solution.py:372
  75.6 42.6 %collective-permute-start.12 = (bf16[8,256,128]{2,1,0:T(8,128)(2,1)S(1)}, bf16[8,256,128]{2,1,0:T(8,128)(2,1)}, u32[]{:S(2)}, u32[]{:S(2)}) collective-permute-start(bf16[8,256,128]{2,1,0:T(8,128)(2,1)S(1)} %collective-permute-done.11.refs_15_), channel_id=1, source_target_pairs={{6,0},{0,2},{2,4},{4,6},{7,1},{1,3},{3,5},{5,7},{14,8},{8,10},{10,... | collective-permute-start | bytes 1572872 | tf_op jit(solution)/shard_map/ppermute | solution.py:372
  86.8 31.3 %collective-permute-start.21 = (bf16[8,256,128]{2,1,0:T(8,128)(2,1)S(1)}, bf16[8,256,128]{2,1,0:T(8,128)(2,1)}, u32[]{:S(2)}, u32[]{:S(2)}) collective-permute-start(bf16[8,256,128]{2,1,0:T(8,128)(2,1)S(1)} %collective-permute-done.20.refs_23_), channel_id=1, source_target_pairs={{24,0},{0,8},{8,16},{16,24},{25,1},{1,9},{9,17},{17,25},{26,2},{2,... | collective-permute-start | bytes 1572872 | tf_op jit(solution)/shard_map/ppermute | solution.py:372
  86.8 31.4 %collective-permute-start.10 = (bf16[8,256,128]{2,1,0:T(8,128)(2,1)}, bf16[8,256,128]{2,1,0:T(8,128)(2,1)}, u32[]{:S(2)}, u32[]{:S(2)}) collective-permute-start(bf16[8,256,128]{2,1,0:T(8,128)(2,1)} %collective-permute-done.8.refs_10_), channel_id=1, source_target_pairs={{2,0},{4,2},{6,4},{0,6},{3,1},{5,3},{7,5},{1,7},{10,8},{12,10},{14... | collective-permute-start | bytes 1572872 | tf_op jit(solution)/shard_map/ppermute | solution.py:372
  90.4 27.8 %collective-permute-start.19 = (bf16[8,256,128]{2,1,0:T(8,128)(2,1)}, bf16[8,256,128]{2,1,0:T(8,128)(2,1)}, u32[]{:S(2)}, u32[]{:S(2)}) collective-permute-start(bf16[8,256,128]{2,1,0:T(8,128)(2,1)} %collective-permute-done.17.refs_18_), channel_id=1, source_target_pairs={{8,0},{16,8},{24,16},{0,24},{9,1},{17,9},{25,17},{1,25},{10,2},{18... | collective-permute-start | bytes 1572872 | tf_op jit(solution)/shard_map/ppermute | solution.py:372
  130.5 20.5 %collective-permute-start.23 = (bf16[256,1024]{1,0:T(8,128)(2,1)}, bf16[256,1024]{1,0:T(8,128)(2,1)S(1)}, u32[]{:S(2)}, u32[]{:S(2)}) collective-permute-start(bf16[256,1024]{1,0:T(8,128)(2,1)} %get-tuple-element.26), channel_id=1, source_target_pairs={{0,32},{32,0},{64,96},{96,64},{1,33},{33,1},{65,97},{97,65},{2,34}... | collective-permute-start | bytes 1572872 | tf_op jit(solution)/shard_map/ppermute | solution.py:423
  147.5 15.2 %collective-permute-start.24 = (bf16[256,1024]{1,0:T(8,128)(2,1)}, bf16[256,1024]{1,0:T(8,128)(2,1)S(1)}, u32[]{:S(2)}, u32[]{:S(2)}) collective-permute-start(bf16[256,1024]{1,0:T(8,128)(2,1)} %get-tuple-element.27), channel_id=1, source_target_pairs={{0,64},{32,96},{64,0},{96,32},{1,65},{33,97},{65,1},{97,33},{2,66}... | collective-permute-start | bytes 1572872 | tf_op jit(solution)/shard_map/ppermute | solution.py:423
  150.3 23.8 %collective-permute-start.25 = (bf16[256,1024]{1,0:T(8,128)(2,1)}, bf16[256,1024]{1,0:T(8,128)(2,1)S(1)}, u32[]{:S(2)}, u32[]{:S(2)}) collective-permute-start(bf16[256,1024]{1,0:T(8,128)(2,1)} %get-tuple-element.28), channel_id=1, source_target_pairs={{0,96},{32,64},{64,32},{96,0},{1,97},{33,65},{65,33},{97,1},{2,98}... | collective-permute-start | bytes 1572872 | tf_op jit(solution)/shard_map/ppermute | solution.py:423
  (11 other events, 143.9 us)

commit v3 on v2

--- a/solution.py
+++ b/solution.py
@@ -107,7 +107,7 @@
 
 
 def near_kernel(first_head, slash_ref, base_ref, q_ref, next_q_ref, far_ref, third_ref, second_ref, first_ref, own_ref, *refs):
-    near_ref, stat_ref, band, score_a, score_b, top_a, top_b, sems = refs[-8:]
+    near_ref, stat_ref, band, score_a, score_b, top_a, top_b = refs[-7:]
     head = first_head + pl.program_id(0)
     last_head = first_head + pl.num_programs(0) - 1
     slab_blocks = own_ref.shape[0]
@@ -144,15 +144,11 @@
         if first_head:
             stat_ref[...] = refs[1][...]
         start = 0
-        copies = []
-        far = far_ref.at[pl.ds(slab_blocks - REACH % slab_blocks, REACH % slab_blocks)]
-        for number, part in enumerate((far, third_ref, second_ref, first_ref, own_ref)):
-            copies.append(pltpu.make_async_copy(part, band.at[pl.ds(start, part.shape[0])], sems.at[number]))
-            start += part.shape[0]
-        for copy in copies:
-            copy.start()
-        for copy in copies:
-            copy.wait()
+        for part in (far_ref, third_ref, second_ref, first_ref, own_ref):
+            skipped = slab_blocks - REACH % slab_blocks if start == 0 else 0
+            length = slab_blocks - skipped
+            band[start : start + length] = part[skipped:]
+            start += length
         begin(q_ref, 0, offsets)
 
     for index in range(slab_blocks):
@@ -179,7 +175,7 @@
                 pl.BlockSpec((rows, HD), lambda h, *_: (0, first_head + h)),
                 pl.BlockSpec((BLK, HD), lambda h, *_: (0, jnp.minimum(first_head + h + 1, heads.stop - 1))),
             ]
-            + [hbm] * 5
+            + [pl.BlockSpec(memory_space=pltpu.VMEM)] * 5
             + [hbm, pl.BlockSpec((rows, HD), lambda h, *_: (0, 0))][: len(done)],
             out_specs=[
                 pl.BlockSpec((rows, HD), lambda h, *_: (0, first_head + h)),
@@ -191,7 +187,6 @@
                 pltpu.VMEM((BLK, (slash_count + 1) * BLK), jnp.float32),
                 pltpu.VMEM((BLK, HD), jnp.float32),
                 pltpu.VMEM((BLK, HD), jnp.float32),
-                pltpu.SemaphoreType.DMA((5,)),
             ],
         ),
         out_shape=[

time: 176 us -> 174 us (0.989)
  transfers between devices with their start and end apart: 26 -> 26, of which waited for: 8 -> 8; matrix products, arithmetic and copies ran while one was open for 7% -> 7% of each run, Pallas kernels for 21% -> 20%
where the time goes in v3:
time: 174 us
  starting transfers between devices  54.7 us (31%)
  waiting for transfers between devices  54.5 us (31%)
  Pallas kernels  50.8 us (29%)
  other arithmetic  9.79 us (6%)
  local copies, waits for them, and re-layouts  3.46 us (2%)
    ppermute x18, starting transfers between devices, from_ahead(): lax.ppermute(array, axis, [((i + by) % size, i) for i in range(size)])  38.3 us
    pallas_call x2, Pallas kernels, vertical_quarters(): pl.pallas_call(functools.partial(vertical_kernel, count, quarter_count, l...  24.6 us
    ppermute x3, waiting for transfers between devices, sent(): return lax.ppermute(piece, 'head', [(i, i ^ step) for i in range(parts)])  23 us
    pallas_call x2, Pallas kernels, near(): pl.pallas_call(functools.partial(near_kernel, first_head), grid_spec=pltp...  22.9 us
    ppermute x18, waiting for transfers between devices, from_ahead(): lax.ppermute(array, axis, [((i + by) % size, i) for i in range(size)])  15.9 us
    ppermute x2, waiting for transfers between devices, from_before(): lax.ppermute(array, SEQ, [(i, (i + pairs * pair) % slabs) for i in range(...  13.1 us
    ppermute x3, starting transfers between devices, sent(): return lax.ppermute(piece, 'head', [(i, i ^ step) for i in range(parts)])  7.81 us
    ppermute x2, starting transfers between devices, from_before(): lax.ppermute(array, SEQ, [(i, (i + pairs * pair) % slabs) for i in range(...  5.76 us
  transfers between devices with their start and end apart: 26, of which 8 were waited for; matrix products, arithmetic and copies ran while one was open for 7% of the time, Pallas kernels for 20%

profile of v3, /device:TPU:1, one launch (start us, length us, event | category | flops | bytes accessed | tf_op | source)
XLA Modules:
  0.0 173.7 jit_solution(12857243377700045575)
XLA Ops:
  0.0 3.3 %prep.1 = (bf16[8,256,128]{2,1,0:T(8,128)(2,1)}, bf16[4,256,128]{2,1,0:T(8,128)(2,1)}) custom-call(s32[8,8]{1,0:T(8,128)} %vertical_ref.1, s32[1]{0:T(128)} %bitcast.2.base_ref, bf16[1024,128]{1,0:T(8,128)(2,1)} %keys_ref.1, bf16[1024,128]{1,0:T(8,128)(2,1)} %values_ref.1), custom_call_target="tpu_custom_call" | custom-call | tf_op jit(solution)/shard_map/prep/pallas_call | solution.py:53
  3.3 2.5 %collective-permute-start.1 = (bf16[8,256,128]{2,1,0:T(8,128)(2,1)}, bf16[8,256,128]{2,1,0:T(8,128)(2,1)S(1)}, u32[]{:S(2)}, u32[]{:S(2)}) collective-permute-start(bf16[8,256,128]{2,1,0:T(8,128)(2,1)} %get-tuple-element.17.own_ref), channel_id=1, source_target_pairs={{0,2},{1,3},{2,4},{3,5},{4,6},{5,7},{6,8},{7,9},{8,10},{9,11},{10,... | collective-permute-start | bytes 1572872 | tf_op jit(solution)/shard_map/ppermute | solution.py:395
  5.7 3.3 %collective-permute-start = (bf16[8,256,128]{2,1,0:T(8,128)(2,1)}, bf16[8,256,128]{2,1,0:T(8,128)(2,1)S(1)}, u32[]{:S(2)}, u32[]{:S(2)}) collective-permute-start(bf16[8,256,128]{2,1,0:T(8,128)(2,1)} %get-tuple-element.17.own_ref), channel_id=1, source_target_pairs={{0,4},{1,5},{2,6},{3,7},{4,8},{5,9},{6,10},{7,11},{8,12},{9,13},{1... | collective-permute-start | bytes 1572872 | tf_op jit(solution)/shard_map/ppermute | solution.py:395
  9.0 1.3 collective-permute-start.4
  10.3 1.0 fusion.12
  13.5 2.4 %collective-permute-done.4 = bf16[4,256,128]{2,1,0:T(8,128)(2,1)S(1)} collective-permute-done((bf16[4,256,128]{2,1,0:T(8,128)(2,1)}, bf16[4,256,128]{2,1,0:T(8,128)(2,1)S(1)}, u32[]{:S(2)}, u32[]{:S(2)}) %collective-permute-start.4) | collective-permute-done | bytes 262176 | tf_op jit(solution)/shard_map/ppermute | solution.py:392
  15.9 2.8 %collective-permute-start.6 = (bf16[4,256,128]{2,1,0:T(8,128)(2,1)S(1)}, bf16[4,256,128]{2,1,0:T(8,128)(2,1)S(1)}, u32[]{:S(2)}, u32[]{:S(2)}) collective-permute-start(bf16[4,256,128]{2,1,0:T(8,128)(2,1)S(1)} %pad_maximum_fusion.2), channel_id=1, source_target_pairs={{16,0},{24,8},{0,16},{8,24},{17,1},{25,9},{1,17},{9,25},{18,2},{26... | collective-permute-start | bytes 786440 | tf_op jit(solution)/shard_map/ppermute | solution.py:367
  19.5 11.0 %collective-permute-done.1.second_ref = bf16[8,256,128]{2,1,0:T(8,128)(2,1)S(1)} collective-permute-done((bf16[8,256,128]{2,1,0:T(8,128)(2,1)}, bf16[8,256,128]{2,1,0:T(8,128)(2,1)S(1)}, u32[]{:S(2)}, u32[]{:S(2)}) %collective-permute-start.1) | collective-permute-done | bytes 524320 | tf_op jit(solution)/shard_map/ppermute | solution.py:395
  30.5 2.1 %collective-permute-done.far_ref = bf16[8,256,128]{2,1,0:T(8,128)(2,1)S(1)} collective-permute-done((bf16[8,256,128]{2,1,0:T(8,128)(2,1)}, bf16[8,256,128]{2,1,0:T(8,128)(2,1)S(1)}, u32[]{:S(2)}, u32[]{:S(2)}) %collective-permute-start) | collective-permute-done | bytes 524320 | tf_op jit(solution)/shard_map/ppermute | solution.py:395
  34.8 1.3 collective-permute-start.2
  36.4 3.2 %collective-permute-done.15 = bf16[4,256,128]{2,1,0:T(8,128)(2,1)S(1)} collective-permute-done((bf16[4,256,128]{2,1,0:T(8,128)(2,1)S(1)}, bf16[4,256,128]{2,1,0:T(8,128)(2,1)S(1)}, u32[]{:S(2)}, u32[]{:S(2)}) %collective-permute-start.15) | collective-permute-done | bytes 262176 | tf_op jit(solution)/shard_map/ppermute | solution.py:367
  39.6 7.9 %collective-permute-start.11 = (bf16[8,256,128]{2,1,0:T(8,128)(2,1)S(1)}, bf16[8,256,128]{2,1,0:T(8,128)(2,1)S(1)}, u32[]{:S(2)}, u32[]{:S(2)}) collective-permute-start(bf16[8,256,128]{2,1,0:T(8,128)(2,1)S(1)} %constant_dynamic-update-slice_fusion.refs_9_), channel_id=1, source_target_pairs={{6,0},{0,2},{2,4},{4,6},{7,1},{1,3},{3,5},{5,7},{14,8},{8,10},{10,... | collective-permute-start | bytes 1572872 | tf_op jit(solution)/shard_map/ppermute | solution.py:367
  47.7 1.3 compare_reduce_fusion
  48.9 7.2 %collective-permute-start.14 = (bf16[4,256,128]{2,1,0:T(8,128)(2,1)S(1)}, bf16[4,256,128]{2,1,0:T(8,128)(2,1)}, u32[]{:S(2)}, u32[]{:S(2)}) collective-permute-start(bf16[4,256,128]{2,1,0:T(8,128)(2,1)S(1)} %pad_maximum_fusion.3), channel_id=1, source_target_pairs={{2,0},{4,2},{6,4},{0,6},{3,1},{5,3},{7,5},{1,7},{10,8},{12,10},{14... | collective-permute-start | bytes 786440 | tf_op jit(solution)/shard_map/ppermute | solution.py:367
  57.2 1.0 pad_maximum_fusion.refs_8_
  58.2 1.9 %collective-permute-done.14 = bf16[4,256,128]{2,1,0:T(8,128)(2,1)} collective-permute-done((bf16[4,256,128]{2,1,0:T(8,128)(2,1)S(1)}, bf16[4,256,128]{2,1,0:T(8,128)(2,1)}, u32[]{:S(2)}, u32[]{:S(2)}) %collective-permute-start.14) | collective-permute-done | bytes 262176 | tf_op jit(solution)/shard_map/ppermute | solution.py:367
  60.1 2.2 %collective-permute-start.18 = (bf16[8,256,128]{2,1,0:T(8,128)(2,1)S(1)}, bf16[8,256,128]{2,1,0:T(8,128)(2,1)S(1)}, u32[]{:S(2)}, u32[]{:S(2)}) collective-permute-start(bf16[8,256,128]{2,1,0:T(8,128)(2,1)S(1)} %constant_dynamic-update-slice_fusion.2.refs_17_), channel_id=1, source_target_pairs={{8,0},{16,8},{24,16},{0,24},{9,1},{17,9},{25,17},{1,25},{10,2},{18... | collective-permute-start | bytes 1572872 | tf_op jit(solution)/shard_map/ppermute | solution.py:367
  62.3 1.0 pad_maximum_fusion.1.refs_16_
  63.3 3.6 %collective-permute-start.9 = (bf16[8,256,128]{2,1,0:T(8,128)(2,1)S(1)}, bf16[8,256,128]{2,1,0:T(8,128)(2,1)S(1)}, u32[]{:S(2)}, u32[]{:S(2)}) collective-permute-start(bf16[8,256,128]{2,1,0:T(8,128)(2,1)S(1)} %constant_dynamic-update-slice_fusion.refs_9_), channel_id=1, source_target_pairs={{2,0},{4,2},{6,4},{0,6},{3,1},{5,3},{7,5},{1,7},{10,8},{12,10},{14... | collective-permute-start | bytes 1572872 | tf_op jit(solution)/shard_map/ppermute | solution.py:367
  66.9 5.1 %collective-permute-start.8 = (bf16[8,256,128]{2,1,0:T(8,128)(2,1)S(1)}, bf16[8,256,128]{2,1,0:T(8,128)(2,1)}, u32[]{:S(2)}, u32[]{:S(2)}) collective-permute-start(bf16[8,256,128]{2,1,0:T(8,128)(2,1)S(1)} %pad_maximum_fusion.refs_8_), channel_id=1, source_target_pairs={{2,0},{4,2},{6,4},{0,6},{3,1},{5,3},{7,5},{1,7},{10,8},{12,10},{14... | collective-permute-start | bytes 1572872 | tf_op jit(solution)/shard_map/ppermute | solution.py:367
  74.2 1.4 collective-permute-start.22
  76.0 10.9 %collective-permute-done.8.refs_10_ = bf16[8,256,128]{2,1,0:T(8,128)(2,1)} collective-permute-done((bf16[8,256,128]{2,1,0:T(8,128)(2,1)S(1)}, bf16[8,256,128]{2,1,0:T(8,128)(2,1)}, u32[]{:S(2)}, u32[]{:S(2)}) %collective-permute-start.8) | collective-permute-done | bytes 524320 | tf_op jit(solution)/shard_map/ppermute | solution.py:367
  86.8 3.5 %collective-permute-start.10 = (bf16[8,256,128]{2,1,0:T(8,128)(2,1)}, bf16[8,256,128]{2,1,0:T(8,128)(2,1)}, u32[]{:S(2)}, u32[]{:S(2)}) collective-permute-start(bf16[8,256,128]{2,1,0:T(8,128)(2,1)} %collective-permute-done.8.refs_10_), channel_id=1, source_target_pairs={{2,0},{4,2},{6,4},{0,6},{3,1},{5,3},{7,5},{1,7},{10,8},{12,10},{14... | collective-permute-start | bytes 1572872 | tf_op jit(solution)/shard_map/ppermute | solution.py:367
  90.4 2.9 %collective-permute-start.19 = (bf16[8,256,128]{2,1,0:T(8,128)(2,1)}, bf16[8,256,128]{2,1,0:T(8,128)(2,1)}, u32[]{:S(2)}, u32[]{:S(2)}) collective-permute-start(bf16[8,256,128]{2,1,0:T(8,128)(2,1)} %collective-permute-done.17.refs_18_), channel_id=1, source_target_pairs={{8,0},{16,8},{24,16},{0,24},{9,1},{17,9},{25,17},{1,25},{10,2},{18... | collective-permute-start | bytes 1572872 | tf_op jit(solution)/shard_map/ppermute | solution.py:367
  93.9 11.3 %near.2 = (f32[1024,1024]{1,0:T(8,128)}, f32[1024,128]{1,0:T(8,128)}) custom-call(s32[8,8]{1,0:T(8,128)} %slash_ref.3, s32[1]{0:T(128)} %bitcast.2.base_ref, bf16[1024,1024]{1,0:T(8,128)(2,1)} %refs_5_.3, bf16[1024,1024]{1,0:T(8,128)(2,1)} %refs_5_.3, bf16[8,256,128]{2,1,0:T(8,128)(2,1)} %copy-done.12, ...), custom_call_target="tpu_custom_call" | custom-call | flops 2415919104 | bytes 4194304 | tf_op jit(solution)/shard_map/near/pallas_call | solution.py:169
  105.3 11.6 %near.3 = (f32[1024,1024]{1,0:T(8,128)}, f32[1024,128]{1,0:T(8,128)}) custom-call(s32[8,8]{1,0:T(8,128)} %slash_ref.3, s32[1]{0:T(128)} %bitcast.2.base_ref, bf16[1024,1024]{1,0:T(8,128)(2,1)} %refs_5_.3, bf16[1024,1024]{1,0:T(8,128)(2,1)} %refs_5_.3, bf16[8,256,128]{2,1,0:T(8,128)(2,1)} %copy-done.12, ...), custom_call_target="tpu_custom_call", output_to_operand_aliasing={{0}: (9, {})} | custom-call | flops 2415919104 | bytes 4194304 | tf_op jit(solution)/shard_map/near/pallas_call | solution.py:169
  116.9 12.3 %vertical.2 = (bf16[256,1024]{1,0:T(8,128)(2,1)}, bf16[256,1024]{1,0:T(8,128)(2,1)}) custom-call(s32[64]{0:T(128)} %fusion.5.slot_ref, s32[8,64]{1,0:T(8,128)} %fusion.4.ok_ref, s32[2]{0:T(128)} %get-tuple-element.33.quarters_ref, bf16[1024,1024]{1,0:T(8,128)(2,1)} %refs_5_.3, bf16[1024,1024]{1,0:T(8,128)(2,1)} %refs_5_.3, ...), custom_call_target="tpu_custom_call" | custom-call | flops 2147483648 | bytes 8388608 | tf_op jit(solution)/shard_map/vertical/pallas_call | solution.py:323
  129.3 4.6 %collective-permute-start.23 = (bf16[256,1024]{1,0:T(8,128)(2,1)}, bf16[256,1024]{1,0:T(8,128)(2,1)S(1)}, u32[]{:S(2)}, u32[]{:S(2)}) collective-permute-start(bf16[256,1024]{1,0:T(8,128)(2,1)} %get-tuple-element.26), channel_id=1, source_target_pairs={{0,32},{32,0},{64,96},{96,64},{1,33},{33,1},{65,97},{97,65},{2,34}... | collective-permute-start | bytes 1572872 | tf_op jit(solution)/shard_map/ppermute | solution.py:418
  133.8 12.3 %vertical.3 = (bf16[256,1024]{1,0:T(8,128)(2,1)}, bf16[256,1024]{1,0:T(8,128)(2,1)}) custom-call(s32[64]{0:T(128)} %fusion.5.slot_ref, s32[8,64]{1,0:T(8,128)} %fusion.4.ok_ref, s32[2]{0:T(128)} %get-tuple-element.34.quarters_ref, bf16[1024,1024]{1,0:T(8,128)(2,1)} %refs_5_.3, bf16[1024,1024]{1,0:T(8,128)(2,1)} %refs_5_.3, ...), custom_call_target="tpu_custom_call" | custom-call | flops 2147483648 | bytes 8388608 | tf_op jit(solution)/shard_map/vertical/pallas_call | solution.py:323
  146.2 2.9 %collective-permute-start.24 = (bf16[256,1024]{1,0:T(8,128)(2,1)}, bf16[256,1024]{1,0:T(8,128)(2,1)S(1)}, u32[]{:S(2)}, u32[]{:S(2)}) collective-permute-start(bf16[256,1024]{1,0:T(8,128)(2,1)} %get-tuple-element.27), channel_id=1, source_target_pairs={{0,64},{32,96},{64,0},{96,32},{1,65},{33,97},{65,1},{97,33},{2,66}... | collective-permute-start | bytes 1572872 | tf_op jit(solution)/shard_map/ppermute | solution.py:418
  149.8 11.6 %collective-permute-done.24 = bf16[256,1024]{1,0:T(8,128)(2,1)S(1)} collective-permute-done((bf16[256,1024]{1,0:T(8,128)(2,1)}, bf16[256,1024]{1,0:T(8,128)(2,1)S(1)}, u32[]{:S(2)}, u32[]{:S(2)}) %collective-permute-start.24) | collective-permute-done | bytes 524320 | tf_op jit(solution)/shard_map/ppermute | solution.py:418
  161.5 11.4 %collective-permute-done.25 = bf16[256,1024]{1,0:T(8,128)(2,1)S(1)} collective-permute-done((bf16[256,1024]{1,0:T(8,128)(2,1)}, bf16[256,1024]{1,0:T(8,128)(2,1)S(1)}, u32[]{:S(2)}, u32[]{:S(2)}) %collective-permute-start.25) | collective-permute-done | bytes 524320 | tf_op jit(solution)/shard_map/ppermute | solution.py:418
  (93 shorter events, 11.3 us)
Async XLA Ops:
  3.3 27.2 %collective-permute-start.1 = (bf16[8,256,128]{2,1,0:T(8,128)(2,1)}, bf16[8,256,128]{2,1,0:T(8,128)(2,1)S(1)}, u32[]{:S(2)}, u32[]{:S(2)}) collective-permute-start(bf16[8,256,128]{2,1,0:T(8,128)(2,1)} %get-tuple-element.17.own_ref), channel_id=1, source_target_pairs={{0,2},{1,3},{2,4},{3,5},{4,6},{5,7},{6,8},{7,9},{8,10},{9,11},{10,... | collective-permute-start | bytes 1572872 | tf_op jit(solution)/shard_map/ppermute | solution.py:395
  5.7 26.9 %collective-permute-start = (bf16[8,256,128]{2,1,0:T(8,128)(2,1)}, bf16[8,256,128]{2,1,0:T(8,128)(2,1)S(1)}, u32[]{:S(2)}, u32[]{:S(2)}) collective-permute-start(bf16[8,256,128]{2,1,0:T(8,128)(2,1)} %get-tuple-element.17.own_ref), channel_id=1, source_target_pairs={{0,4},{1,5},{2,6},{3,7},{4,8},{5,9},{6,10},{7,11},{8,12},{9,13},{1... | collective-permute-start | bytes 1572872 | tf_op jit(solution)/shard_map/ppermute | solution.py:395
  9.0 6.9 %collective-permute-start.4 = (bf16[4,256,128]{2,1,0:T(8,128)(2,1)}, bf16[4,256,128]{2,1,0:T(8,128)(2,1)S(1)}, u32[]{:S(2)}, u32[]{:S(2)}) collective-permute-start(bf16[4,256,128]{2,1,0:T(8,128)(2,1)} %get-tuple-element.24), channel_id=1, source_target_pairs={{0,1},{1,0},{2,3},{3,2},{4,5},{5,4},{6,7},{7,6},{8,9},{9,8},{10,11... | collective-permute-start | bytes 786440 | tf_op jit(solution)/shard_map/ppermute | solution.py:392
  15.9 18.8 %collective-permute-start.6 = (bf16[4,256,128]{2,1,0:T(8,128)(2,1)S(1)}, bf16[4,256,128]{2,1,0:T(8,128)(2,1)S(1)}, u32[]{:S(2)}, u32[]{:S(2)}) collective-permute-start(bf16[4,256,128]{2,1,0:T(8,128)(2,1)S(1)} %pad_maximum_fusion.2), channel_id=1, source_target_pairs={{16,0},{24,8},{0,16},{8,24},{17,1},{25,9},{1,17},{9,25},{18,2},{26... | collective-permute-start | bytes 786440 | tf_op jit(solution)/shard_map/ppermute | solution.py:367
  18.7 17.3 %collective-permute-start.7 = (bf16[4,256,128]{2,1,0:T(8,128)(2,1)S(1)}, bf16[4,256,128]{2,1,0:T(8,128)(2,1)S(1)}, u32[]{:S(2)}, u32[]{:S(2)}) collective-permute-start(bf16[4,256,128]{2,1,0:T(8,128)(2,1)S(1)} %pad_maximum_fusion.2), channel_id=1, source_target_pairs={{24,0},{0,8},{8,16},{16,24},{25,1},{1,9},{9,17},{17,25},{26,2},{2,... | collective-permute-start | bytes 786440 | tf_op jit(solution)/shard_map/ppermute | solution.py:367
  19.1 20.5 %collective-permute-start.15 = (bf16[4,256,128]{2,1,0:T(8,128)(2,1)S(1)}, bf16[4,256,128]{2,1,0:T(8,128)(2,1)S(1)}, u32[]{:S(2)}, u32[]{:S(2)}) collective-permute-start(bf16[4,256,128]{2,1,0:T(8,128)(2,1)S(1)} %pad_maximum_fusion.3), channel_id=1, source_target_pairs={{4,0},{6,2},{0,4},{2,6},{5,1},{7,3},{1,5},{3,7},{12,8},{14,10},{8,... | collective-permute-start | bytes 786440 | tf_op jit(solution)/shard_map/ppermute | solution.py:367
  30.5 17.1 %collective-permute-start.16 = (bf16[4,256,128]{2,1,0:T(8,128)(2,1)S(1)}, bf16[4,256,128]{2,1,0:T(8,128)(2,1)S(1)}, u32[]{:S(2)}, u32[]{:S(2)}) collective-permute-start(bf16[4,256,128]{2,1,0:T(8,128)(2,1)S(1)} %pad_maximum_fusion.3), channel_id=1, source_target_pairs={{6,0},{0,2},{2,4},{4,6},{7,1},{1,3},{3,5},{5,7},{14,8},{8,10},{10,... | collective-permute-start | bytes 786440 | tf_op jit(solution)/shard_map/ppermute | solution.py:367
  32.6 16.3 %collective-permute-start.5 = (bf16[4,256,128]{2,1,0:T(8,128)(2,1)S(1)}, bf16[4,256,128]{2,1,0:T(8,128)(2,1)}, u32[]{:S(2)}, u32[]{:S(2)}) collective-permute-start(bf16[4,256,128]{2,1,0:T(8,128)(2,1)S(1)} %pad_maximum_fusion.2), channel_id=1, source_target_pairs={{8,0},{16,8},{24,16},{0,24},{9,1},{17,9},{25,17},{1,25},{10,2},{18... | collective-permute-start | bytes 786440 | tf_op jit(solution)/shard_map/ppermute | solution.py:367
  34.8 28.5 %collective-permute-start.2 = (bf16[8,256,128]{2,1,0:T(8,128)(2,1)}, bf16[8,256,128]{2,1,0:T(8,128)(2,1)}, u32[]{:S(2)}, u32[]{:S(2)}) collective-permute-start(bf16[8,256,128]{2,1,0:T(8,128)(2,1)} %broadcast_select_fusion.1), channel_id=1, source_target_pairs={{0,1},{1,0},{2,3},{3,2},{4,5},{5,4},{6,7},{7,6},{8,9},{9,8},{10,11... | collective-permute-start | bytes 1572872 | tf_op jit(solution)/shard_map/ppermute | solution.py:392
  36.1 30.8 %collective-permute-start.3 = (bf16[8,256,128]{2,1,0:T(8,128)(2,1)}, bf16[8,256,128]{2,1,0:T(8,128)(2,1)}, u32[]{:S(2)}, u32[]{:S(2)}) collective-permute-start(bf16[8,256,128]{2,1,0:T(8,128)(2,1)} %broadcast_select_fusion), channel_id=1, source_target_pairs={{0,1},{1,0},{2,3},{3,2},{4,5},{5,4},{6,7},{7,6},{8,9},{9,8},{10,11... | collective-permute-start | bytes 1572872 | tf_op jit(solution)/shard_map/ppermute | solution.py:392
  36.4 68.8 %copy-start.3 = (bf16[8,256,128]{2,1,0:T(8,128)(2,1)}, bf16[8,256,128]{2,1,0:T(8,128)(2,1)S(1)}, u32[]{:S(2)}) copy-start(bf16[8,256,128]{2,1,0:T(8,128)(2,1)S(1)} %constant_dynamic-update-slice_fusion.refs_9_) | copy-start | bytes 1572868
  39.6 32.4 %collective-permute-start.11 = (bf16[8,256,128]{2,1,0:T(8,128)(2,1)S(1)}, bf16[8,256,128]{2,1,0:T(8,128)(2,1)S(1)}, u32[]{:S(2)}, u32[]{:S(2)}) collective-permute-start(bf16[8,256,128]{2,1,0:T(8,128)(2,1)S(1)} %constant_dynamic-update-slice_fusion.refs_9_), channel_id=1, source_target_pairs={{6,0},{0,2},{2,4},{4,6},{7,1},{1,3},{3,5},{5,7},{14,8},{8,10},{10,... | collective-permute-start | bytes 1572872 | tf_op jit(solution)/shard_map/ppermute | solution.py:367
  47.6 57.7 %copy-start.4 = (bf16[8,256,128]{2,1,0:T(8,128)(2,1)}, bf16[8,256,128]{2,1,0:T(8,128)(2,1)S(1)}, u32[]{:S(2)}) copy-start(bf16[8,256,128]{2,1,0:T(8,128)(2,1)S(1)} %constant_dynamic-update-slice_fusion.2.refs_17_) | copy-start | bytes 1572868
  47.6 24.4 %collective-permute-start.20 = (bf16[8,256,128]{2,1,0:T(8,128)(2,1)S(1)}, bf16[8,256,128]{2,1,0:T(8,128)(2,1)S(1)}, u32[]{:S(2)}, u32[]{:S(2)}) collective-permute-start(bf16[8,256,128]{2,1,0:T(8,128)(2,1)S(1)} %constant_dynamic-update-slice_fusion.2.refs_17_), channel_id=1, source_target_pairs={{24,0},{0,8},{8,16},{16,24},{25,1},{1,9},{9,17},{17,25},{26,2},{2,... | collective-permute-start | bytes 1572872 | tf_op jit(solution)/shard_map/ppermute | solution.py:367
  48.9 11.1 %collective-permute-start.14 = (bf16[4,256,128]{2,1,0:T(8,128)(2,1)S(1)}, bf16[4,256,128]{2,1,0:T(8,128)(2,1)}, u32[]{:S(2)}, u32[]{:S(2)}) collective-permute-start(bf16[4,256,128]{2,1,0:T(8,128)(2,1)S(1)} %pad_maximum_fusion.3), channel_id=1, source_target_pairs={{2,0},{4,2},{6,4},{0,6},{3,1},{5,3},{7,5},{1,7},{10,8},{12,10},{14... | collective-permute-start | bytes 786440 | tf_op jit(solution)/shard_map/ppermute | solution.py:367
  58.2 47.1 %copy-start = (bf16[8,256,128]{2,1,0:T(8,128)(2,1)}, bf16[8,256,128]{2,1,0:T(8,128)(2,1)S(1)}, u32[]{:S(2)}) copy-start(bf16[8,256,128]{2,1,0:T(8,128)(2,1)S(1)} %pad_maximum_fusion.refs_8_) | copy-start | bytes 1572868
  60.1 14.1 %collective-permute-start.18 = (bf16[8,256,128]{2,1,0:T(8,128)(2,1)S(1)}, bf16[8,256,128]{2,1,0:T(8,128)(2,1)S(1)}, u32[]{:S(2)}, u32[]{:S(2)}) collective-permute-start(bf16[8,256,128]{2,1,0:T(8,128)(2,1)S(1)} %constant_dynamic-update-slice_fusion.2.refs_17_), channel_id=1, source_target_pairs={{8,0},{16,8},{24,16},{0,24},{9,1},{17,9},{25,17},{1,25},{10,2},{18... | collective-permute-start | bytes 1572872 | tf_op jit(solution)/shard_map/ppermute | solution.py:367
  63.3 42.0 %copy-start.1 = (bf16[8,256,128]{2,1,0:T(8,128)(2,1)}, bf16[8,256,128]{2,1,0:T(8,128)(2,1)S(1)}, u32[]{:S(2)}) copy-start(bf16[8,256,128]{2,1,0:T(8,128)(2,1)S(1)} %pad_maximum_fusion.1.refs_16_) | copy-start | bytes 1572868
  63.3 12.3 %collective-permute-start.9 = (bf16[8,256,128]{2,1,0:T(8,128)(2,1)S(1)}, bf16[8,256,128]{2,1,0:T(8,128)(2,1)S(1)}, u32[]{:S(2)}, u32[]{:S(2)}) collective-permute-start(bf16[8,256,128]{2,1,0:T(8,128)(2,1)S(1)} %constant_dynamic-update-slice_fusion.refs_9_), channel_id=1, source_target_pairs={{2,0},{4,2},{6,4},{0,6},{3,1},{5,3},{7,5},{1,7},{10,8},{12,10},{14... | collective-permute-start | bytes 1572872 | tf_op jit(solution)/shard_map/ppermute | solution.py:367
  66.9 19.9 %collective-permute-start.8 = (bf16[8,256,128]{2,1,0:T(8,128)(2,1)S(1)}, bf16[8,256,128]{2,1,0:T(8,128)(2,1)}, u32[]{:S(2)}, u32[]{:S(2)}) collective-permute-start(bf16[8,256,128]{2,1,0:T(8,128)(2,1)S(1)} %pad_maximum_fusion.refs_8_), channel_id=1, source_target_pairs={{2,0},{4,2},{6,4},{0,6},{3,1},{5,3},{7,5},{1,7},{10,8},{12,10},{14... | collective-permute-start | bytes 1572872 | tf_op jit(solution)/shard_map/ppermute | solution.py:367
  72.0 33.3 %copy-start.5 = (bf16[8,256,128]{2,1,0:T(8,128)(2,1)}, bf16[8,256,128]{2,1,0:T(8,128)(2,1)S(1)}, u32[]{:S(2)}) copy-start(bf16[8,256,128]{2,1,0:T(8,128)(2,1)S(1)} %collective-permute-done.11.refs_15_) | copy-start | bytes 1572868
  72.0 18.3 %collective-permute-start.13 = (bf16[8,256,128]{2,1,0:T(8,128)(2,1)S(1)}, bf16[8,256,128]{2,1,0:T(8,128)(2,1)S(1)}, u32[]{:S(2)}, u32[]{:S(2)}) collective-permute-start(bf16[8,256,128]{2,1,0:T(8,128)(2,1)S(1)} %pad_maximum_fusion.refs_8_), channel_id=1, source_target_pairs={{6,0},{0,2},{2,4},{4,6},{7,1},{1,3},{3,5},{5,7},{14,8},{8,10},{10,... | collective-permute-start | bytes 1572872 | tf_op jit(solution)/shard_map/ppermute | solution.py:367
  72.0 33.3 %copy-start.6 = (bf16[8,256,128]{2,1,0:T(8,128)(2,1)}, bf16[8,256,128]{2,1,0:T(8,128)(2,1)S(1)}, u32[]{:S(2)}) copy-start(bf16[8,256,128]{2,1,0:T(8,128)(2,1)S(1)} %collective-permute-done.20.refs_23_) | copy-start | bytes 1572868
  72.0 14.8 %collective-permute-start.17 = (bf16[8,256,128]{2,1,0:T(8,128)(2,1)S(1)}, bf16[8,256,128]{2,1,0:T(8,128)(2,1)}, u32[]{:S(2)}, u32[]{:S(2)}) collective-permute-start(bf16[8,256,128]{2,1,0:T(8,128)(2,1)S(1)} %pad_maximum_fusion.1.refs_16_), channel_id=1, source_target_pairs={{8,0},{16,8},{24,16},{0,24},{9,1},{17,9},{25,17},{1,25},{10,2},{18... | collective-permute-start | bytes 1572872 | tf_op jit(solution)/shard_map/ppermute | solution.py:367
  74.2 42.7 %collective-permute-start.22 = (bf16[8,256,128]{2,1,0:T(8,128)(2,1)S(1)}, bf16[8,256,128]{2,1,0:T(8,128)(2,1)}, u32[]{:S(2)}, u32[]{:S(2)}) collective-permute-start(bf16[8,256,128]{2,1,0:T(8,128)(2,1)S(1)} %pad_maximum_fusion.1.refs_16_), channel_id=1, source_target_pairs={{24,0},{0,8},{8,16},{16,24},{25,1},{1,9},{9,17},{17,25},{26,2},{2,... | collective-permute-start | bytes 1572872 | tf_op jit(solution)/shard_map/ppermute | solution.py:367
  75.6 41.3 %collective-permute-start.12 = (bf16[8,256,128]{2,1,0:T(8,128)(2,1)S(1)}, bf16[8,256,128]{2,1,0:T(8,128)(2,1)}, u32[]{:S(2)}, u32[]{:S(2)}) collective-permute-start(bf16[8,256,128]{2,1,0:T(8,128)(2,1)S(1)} %collective-permute-done.11.refs_15_), channel_id=1, source_target_pairs={{6,0},{0,2},{2,4},{4,6},{7,1},{1,3},{3,5},{5,7},{14,8},{8,10},{10,... | collective-permute-start | bytes 1572872 | tf_op jit(solution)/shard_map/ppermute | solution.py:367
  86.8 30.1 %collective-permute-start.21 = (bf16[8,256,128]{2,1,0:T(8,128)(2,1)S(1)}, bf16[8,256,128]{2,1,0:T(8,128)(2,1)}, u32[]{:S(2)}, u32[]{:S(2)}) collective-permute-start(bf16[8,256,128]{2,1,0:T(8,128)(2,1)S(1)} %collective-permute-done.20.refs_23_), channel_id=1, source_target_pairs={{24,0},{0,8},{8,16},{16,24},{25,1},{1,9},{9,17},{17,25},{26,2},{2,... | collective-permute-start | bytes 1572872 | tf_op jit(solution)/shard_map/ppermute | solution.py:367
  86.8 30.1 %collective-permute-start.10 = (bf16[8,256,128]{2,1,0:T(8,128)(2,1)}, bf16[8,256,128]{2,1,0:T(8,128)(2,1)}, u32[]{:S(2)}, u32[]{:S(2)}) collective-permute-start(bf16[8,256,128]{2,1,0:T(8,128)(2,1)} %collective-permute-done.8.refs_10_), channel_id=1, source_target_pairs={{2,0},{4,2},{6,4},{0,6},{3,1},{5,3},{7,5},{1,7},{10,8},{12,10},{14... | collective-permute-start | bytes 1572872 | tf_op jit(solution)/shard_map/ppermute | solution.py:367
  90.4 26.6 %collective-permute-start.19 = (bf16[8,256,128]{2,1,0:T(8,128)(2,1)}, bf16[8,256,128]{2,1,0:T(8,128)(2,1)}, u32[]{:S(2)}, u32[]{:S(2)}) collective-permute-start(bf16[8,256,128]{2,1,0:T(8,128)(2,1)} %collective-permute-done.17.refs_18_), channel_id=1, source_target_pairs={{8,0},{16,8},{24,16},{0,24},{9,1},{17,9},{25,17},{1,25},{10,2},{18... | collective-permute-start | bytes 1572872 | tf_op jit(solution)/shard_map/ppermute | solution.py:367
  129.3 20.4 %collective-permute-start.23 = (bf16[256,1024]{1,0:T(8,128)(2,1)}, bf16[256,1024]{1,0:T(8,128)(2,1)S(1)}, u32[]{:S(2)}, u32[]{:S(2)}) collective-permute-start(bf16[256,1024]{1,0:T(8,128)(2,1)} %get-tuple-element.26), channel_id=1, source_target_pairs={{0,32},{32,0},{64,96},{96,64},{1,33},{33,1},{65,97},{97,65},{2,34}... | collective-permute-start | bytes 1572872 | tf_op jit(solution)/shard_map/ppermute | solution.py:418
  146.2 15.2 %collective-permute-start.24 = (bf16[256,1024]{1,0:T(8,128)(2,1)}, bf16[256,1024]{1,0:T(8,128)(2,1)S(1)}, u32[]{:S(2)}, u32[]{:S(2)}) collective-permute-start(bf16[256,1024]{1,0:T(8,128)(2,1)} %get-tuple-element.27), channel_id=1, source_target_pairs={{0,64},{32,96},{64,0},{96,32},{1,65},{33,97},{65,1},{97,33},{2,66}... | collective-permute-start | bytes 1572872 | tf_op jit(solution)/shard_map/ppermute | solution.py:418
  149.1 23.8 %collective-permute-start.25 = (bf16[256,1024]{1,0:T(8,128)(2,1)}, bf16[256,1024]{1,0:T(8,128)(2,1)S(1)}, u32[]{:S(2)}, u32[]{:S(2)}) collective-permute-start(bf16[256,1024]{1,0:T(8,128)(2,1)} %get-tuple-element.28), channel_id=1, source_target_pairs={{0,96},{32,64},{64,32},{96,0},{1,97},{33,65},{65,33},{97,1},{2,98}... | collective-permute-start | bytes 1572872 | tf_op jit(solution)/shard_map/ppermute | solution.py:418
  (11 other events, 143.9 us)
